TPU v7x, 32 devices: a whole 2x2x4 slice. The times are simulated.
32 devices in a mesh: win: 8 (over z, y), tile: 4 (over x, core).
Axes of the slice: x: 2, y: 2, z: 4, core: 2. Of those that a mesh axis runs over, the one named last changes fastest.
Arguments:
- right_side: float32 [8, 2, 128, 1024], P('win', None, 'tile'), may hold values from -64 to 64
- error_weight: float32 [8, 2, 128, 1024], P('win', None, 'tile'), may hold values from 0.5 to 4
- coeffs: float32 [4, 8, 2, 128, 1024], P(None, 'win', None, 'tile'), may hold values from 0.1 to 0.4
- obs_block: int32 [8, 128], P('win', 'tile'), may hold values from 0 to 511
- obs_pos: int32 [8, 128, 128], P('win', 'tile'), may hold values from 0 to 127
- obs_weight: float32 [8, 128, 128], P('win', 'tile'), may hold values from 0.5 to 4
Outputs:
- solution_field: float32 [8, 2, 128, 1024], P('win', None, 'tile')
- residual: float32 [8, 2, 128, 1024], P('win', None, 'tile')
All inputs are finite; a program needn't handle non-finite values.
Results may differ from a plain program's by a relative error of at most 0.0001.
Values sent between devices are 32-bit elements; how exact they have to be, the bound alone decides.
A program may use at most 64 MiB of HBM per device.

v0:
```python
import functools

import jax
import jax.numpy as jnp
from jax import lax
from jax.experimental import pallas as pl
from jax.experimental.pallas import tpu as pltpu
from jax.sharding import PartitionSpec as P

ITERS = 3
EDGE = 8


def doubling(length):
    steps, known = [], 1
    while known < length - 1:
        steps.append(known)
        known *= 2
    return steps


def kernel(wins, tiles, rhs, err, cof, oblk_in, opos_in, owgt_in, x_out, r_out,
           obk, ops, owt, v, y, w, wn, c, d, ob, u, ui, vn, z, eo, ei, go, gi, rt, home, tail, part, red,
           x_sem, xs_sem, l_sem, h_send, h_recv, b_send, b_recv, g_send, g_recv,
           rt_send, rt_recv, rd_send, rd_recv, wn_send, wn_recv, hello):
    me_w = lax.axis_index("win")
    me_t = lax.axis_index("tile")
    lev = lax.rem(me_w, 2)
    other = 1 - lev
    mate = me_w + 1 - 2 * lev
    has_next = me_w + 2 < wins
    has_prev = me_w >= 2
    has_north = me_t > 0
    has_south = me_t < tiles - 1
    rows, cols = v.shape[2], v.shape[3]
    oblk, opos, owgt = obk, ops, owt
    count = wins * tiles
    me = me_w * tiles + me_t
    width = opos.shape[2]
    nblk = opos.shape[1]

    def remote(src, dst, ssem, rsem, win, tile):
        return pltpu.make_async_remote_copy(
            src_ref=src, dst_ref=dst, send_sem=ssem, recv_sem=rsem,
            device_id=(win, tile), device_id_type=pl.DeviceIdType.MESH)

    pieces = [(0, EDGE), (rows - EDGE, EDGE)] + [
        (lo, EDGE) for lo in range(EDGE, rows - EDGE, EDGE)]
    many = len(pieces)

    barrier = pltpu.get_barrier_semaphore()

    def signal(sem, win, tile):
        pl.semaphore_signal(sem, inc=1, device_id=(win, tile), device_id_type=pl.DeviceIdType.MESH)

    def greet(sem, ends):
        for there, win, tile in ends:
            pl.when(there)(functools.partial(signal, sem, win, tile))

    def met(sem, ends):
        pl.semaphore_wait(sem, sum(there.astype(jnp.int32) for there, _, _ in ends))

    def along_tile(step):
        return [(me_t >= step, me_w, me_t - step), (me_t + step < tiles, me_w, me_t + step)]

    def along_win(step):
        return [(me_w >= 2 * step, me_w - 2 * step, me_t),
                (me_w + 2 * step < wins, me_w + 2 * step, me_t)]

    facing = [(me_w >= 0, mate, me_t)]
    near = facing + along_tile(1) + along_win(1)
    rounds = ([along_tile(step) for step in doubling(tiles)] + [facing]
              + [along_win(step) for step in doubling(wins // 2)])
    turn = iter(range(len(rounds) + 1))

    def spread():
        at = next(turn, None)
        if at is None:
            return
        if at > 0:
            met(hello.at[at - 1], rounds[at - 1])
        if at < len(rounds):
            greet(hello.at[at], rounds[at])

    greet(barrier, near)

    swaps = [
        remote(rhs.at[0, other], v.at[0, lev], xs_sem.at[0], x_sem.at[0], mate, me_t),
        remote(err.at[0, other], w.at[lev], xs_sem.at[1], x_sem.at[1], mate, me_t),
    ] + [
        remote(cof.at[:, 0, other, pl.ds(lo, n)], c.at[:, lev, pl.ds(lo, n)],
               xs_sem.at[3 + k], x_sem.at[3 + k], mate, me_t)
        for k, (lo, n) in enumerate(pieces)
    ]
    locs = [
        pltpu.make_async_copy(oblk_in, obk, l_sem.at[4]),
        pltpu.make_async_copy(opos_in, ops, l_sem.at[5]),
        pltpu.make_async_copy(owgt_in, owt, l_sem.at[6]),
        pltpu.make_async_copy(rhs.at[0, lev], v.at[0, lev], l_sem.at[0]),
        pltpu.make_async_copy(err.at[0, lev], w.at[lev], l_sem.at[1]),
        pltpu.make_async_copy(rhs.at[0, other], home, l_sem.at[2]),
        pltpu.make_async_copy(cof.at[:, 0, lev], c.at[:, lev], l_sem.at[3]),
    ]
    for s in locs:
        s.start()
    locs = locs[3:] + locs[:3]
    met(barrier, near)
    for s in swaps[:3]:
        s.start()
    spread()

    @pl.when(jnp.logical_not(has_north))
    def _():
        for it in range(ITERS):
            ei[it, 0] = jnp.zeros(ei.shape[2:], jnp.float32)
            gi[it, 0] = jnp.zeros(gi.shape[2:], jnp.float32)

    @pl.when(jnp.logical_not(has_south))
    def _():
        for it in range(ITERS):
            ei[it, 1] = jnp.zeros(ei.shape[2:], jnp.float32)
            gi[it, 1] = jnp.zeros(gi.shape[2:], jnp.float32)

    @pl.when(jnp.logical_not(has_prev))
    def _():
        for it in range(ITERS):
            ui[it] = jnp.zeros(ui.shape[1:], jnp.float32)

    @pl.when(jnp.logical_not(has_next))
    def _():
        wn[...] = jnp.zeros(wn.shape, jnp.float32)
        for it in range(ITERS):
            vn[it] = jnp.zeros(vn.shape[1:], jnp.float32)

    for s in locs[4:]:
        s.wait()
    cell = lax.broadcasted_iota(jnp.int32, (width, width), 0)
    ones = jnp.ones((8, width), jnp.float32)
    ob[lev, nblk:, :] = jnp.zeros((8, width), jnp.float32)

    def per_block(b, carry):
        hit = jnp.where(cell == opos[0, pl.ds(b, 1), :], owgt[0, pl.ds(b, 1), :], 0.0)
        total = lax.dot_general(ones, hit, (((1,), (1,)), ((), ())),
                                precision=lax.Precision.HIGHEST,
                                preferred_element_type=jnp.float32)
        ob[lev, pl.ds(b, 1), :] = total[0:1]
        return carry

    lax.fori_loop(0, nblk, per_block, 0)
    ob[lev, nblk:nblk + 1, 0:nblk] = oblk[...].astype(jnp.float32)
    ob_copy = remote(ob.at[lev], ob.at[lev], xs_sem.at[2], x_sem.at[2], mate, me_t)
    ob_copy.start()
    spread()

    states = (v.at[0], y.at[0], v.at[1])

    def arrived(k):
        return [
            lambda: remote(rhs.at[0, other], v.at[0, other], xs_sem.at[0], x_sem.at[0], mate, me_t),
            lambda: remote(err.at[0, other], w.at[other], xs_sem.at[1], x_sem.at[1], mate, me_t),
        ][k]()


    def edge_copies(out, into, ssem, rsem, it):
        north = remote(out.at[it, 0], into.at[it, 1], ssem.at[it, 0], rsem.at[it, 1],
                       me_w, me_t - 1)
        south = remote(out.at[it, 1], into.at[it, 0], ssem.at[it, 1], rsem.at[it, 0],
                       me_w, me_t + 1)
        return north, south

    def edges_start(out, into, ssem, rsem, it):
        north, south = edge_copies(out, into, ssem, rsem, it)
        pl.when(has_north)(north.start)
        pl.when(has_south)(south.start)

    def edges_wait_recv(out, into, ssem, rsem, it):
        north, south = edge_copies(out, into, ssem, rsem, it)
        pl.when(has_north)(south.wait_recv)
        pl.when(has_south)(north.wait_recv)

    def edges_wait_send(out, into, ssem, rsem, it):
        north, south = edge_copies(out, into, ssem, rsem, it)
        pl.when(has_north)(north.wait_send)
        pl.when(has_south)(south.wait_send)

    def back_copy(it, k):
        lo, n = pieces[k]
        return remote(states[it].at[0, pl.ds(lo, n)], vn.at[it, pl.ds(lo, n)],
                      b_send.at[0, it, k], b_recv.at[0, it, k], me_w - 2, me_t)

    def forth_copy(it, k):
        lo, n = pieces[k]
        return remote(u.at[1, pl.ds(lo, n)], ui.at[it, pl.ds(lo, n)],
                      b_send.at[1, it, k], b_recv.at[1, it, k], me_w + 2, me_t)

    def ret_copy(it):
        return remote(y.at[it, other], rt.at[it], rt_send.at[it], rt_recv.at[it], mate, me_t)

    row = lax.broadcasted_iota(jnp.int32, (rows, cols), 0)
    row8 = lax.broadcasted_iota(jnp.int32, (EDGE, cols), 0)

    def above(a):
        return jnp.where(row == 0, 0.0, pltpu.roll(a, 1, 0))

    def below(a):
        return jnp.where(row == rows - 1, 0.0, pltpu.roll(a, rows - 1, 0))

    def east(a):
        return pltpu.roll(a, cols - 1, 1)

    def west(a):
        return pltpu.roll(a, 1, 1)

    last = rows - 1
    wn_copy = remote(w.at[0], wn, wn_send, wn_recv, me_w - 2, me_t)

    def model_piece(it, i, k):
        lo, n = pieces[k]
        src = states[it]
        a = src[i, lo:lo + n]
        top = ei[it, 0, i:i + 1] if lo == 0 else src[i, lo - 1:lo]
        bottom = ei[it, 1, i:i + 1] if lo + n == rows else src[i, lo + n:lo + n + 1]
        sides = (jnp.where(row8 == 0, top, pltpu.roll(a, 1, 0))
                 + jnp.where(row8 == n - 1, bottom, pltpu.roll(a, n - 1, 0)))
        u[i, lo:lo + n] = (c[0, i, lo:lo + n] * a + c[1, i, lo:lo + n] * sides
                           + c[2, i, lo:lo + n] * east(a) + c[3, i, lo:lo + n] * west(a))

    def sends(it):
        src = states[it]
        for i in range(2):
            eo[it, 0, i:i + 1] = src[i, 0:1]
            eo[it, 1, i:i + 1] = src[i, last:last + 1]
        edges_start(eo, ei, h_send, h_recv, it)

        @pl.when(has_prev)
        def _():
            for k in range(many):
                back_copy(it, k).start()

    def product(it, beside):
        src = states[it]
        sends(it)
        if it > 0:
            beside()
        if it == 0:
            locs[1].wait()
            arrived(1).wait_recv()
            for later in swaps[3:4]:
                later.start()
            pl.when(has_prev)(wn_copy.start)
            locs[3].wait()
            edges_wait_recv(eo, ei, h_send, h_recv, it)
            for k in range(many):
                spread()
                swaps[2 + k].wait_recv()
                for later in swaps[4 + k:5 + k]:
                    later.start()
                model_piece(it, 1, k)
                pl.when(has_next)(forth_copy(it, k).start)
                model_piece(it, 0, k)
                if k == 1:
                    adjoint_edges(it)
                    beside()
        else:
            @pl.when(has_next)
            def _():
                for k in range(many):
                    forth_copy(it - 1, k).wait_send()

            for k in range(2, many):
                model_piece(it, 1, k)
                pl.when(has_next)(forth_copy(it, k).start)
            edges_wait_recv(eo, ei, h_send, h_recv, it)
            for k in range(2):
                model_piece(it, 1, k)
                pl.when(has_next)(forth_copy(it, k).start)
            for k in range(2):
                model_piece(it, 0, k)
            adjoint_edges(it)
            for k in range(2, many):
                model_piece(it, 0, k)

        def adjoint(i, q):
            g = c[1, i] * q
            return (c[0, i] * q + (above(g) + below(g)) + west(c[2, i] * q) + east(c[3, i] * q))

        z[...] = w[1] * (src[1] - u[0])
        y[it, 0] = d[0] * src[0] - adjoint(0, z[...])

        @pl.when(has_next)
        def _():
            for k in range(2, many):
                back_copy(it, k).wait_recv()

        y[it, 1] = (z[...] + d[1] * src[1]) - adjoint(1, wn[...] * (vn[it] - u[1]))

        edges_wait_recv(go, gi, g_send, g_recv, it)
        for i in range(2):
            y[it, i, 0:1] = y[it, i, 0:1] - gi[it, 0, i:i + 1]
            y[it, i, last:last + 1] = y[it, i, last:last + 1] - gi[it, 1, i:i + 1]

        @pl.when(has_prev)
        def _():
            for k in range(many):
                forth_copy(it, k).wait_recv()

        y[it, 0] = y[it, 0] + w[0] * (src[0] - ui[it])

    def adjoint_edges(it):
        src = states[it]

        @pl.when(has_next)
        def _():
            if it == 0:
                wn_copy.wait_recv()
            back_copy(it, 0).wait_recv()
            back_copy(it, 1).wait_recv()

        for side, at in ((0, 0), (1, last)):
            here = slice(at, at + 1)
            go[it, side, 0:1] = c[1, 0, here] * (w[1, here] * (src[1, here] - u[0, here]))
            go[it, side, 1:2] = c[1, 1, here] * (wn[here] * (vn[it, here] - u[1, here]))
        edges_start(go, gi, g_send, g_recv, it)

    def lanes(pair):
        a = jnp.sum(pair[0] + pair[1], axis=0, keepdims=True)
        total = a[:, 0:128]
        for k in range(1, cols // 128):
            total = total + a[:, k * 128:(k + 1) * 128]
        return total

    def reduce_start(it, r, aw):
        part[it, 0:1] = lanes(r * r)
        part[it, 1:2] = lanes(r * aw)

        def send(o, carry):
            to = lax.rem(me + o, count)
            remote(part.at[it], red.at[it, me], rd_send.at[it], rd_recv.at[it],
                   to // tiles, lax.rem(to, tiles)).start()
            return carry

        lax.fori_loop(1, count, send, 0)
        red[it, me] = part[it]

    def reduce_end(it):
        most = red.at[it, pl.ds(0, count - 1)]
        pltpu.make_async_copy(most, most, rd_recv.at[it]).wait()
        total = jnp.sum(red[it], axis=0)
        both = jnp.sum(total, axis=1, keepdims=True)
        return both[0:1], both[1:2]

    locs[0].wait()
    arrived(0).wait_recv()

    def diagonal():
        remote(ob.at[lev], ob.at[other], xs_sem.at[2], x_sem.at[2], mate, me_t).wait_recv()
        per_row = cols // width
        base = lev * (rows * per_row)
        spot = lax.broadcasted_iota(jnp.int32, (rows, nblk), 0) * per_row + base
        for i in range(2):
            who = ob[i, nblk:nblk + 1, 0:nblk]
            sums = ob[i, 0:nblk, :]
            for k in range(per_row):
                hot = jnp.where((spot + k).astype(jnp.float32) == who, 1.0, 0.0)
                d[i, :, k * width:(k + 1) * width] = jnp.dot(
                    hot, sums, precision=lax.Precision.HIGHEST,
                    preferred_element_type=jnp.float32)

    product(0, diagonal)
    for _ in range(len(rounds)):
        spread()

    def first_sums():
        ret_copy(0).start()
        reduce_start(0, v[0], y[0])

    product(1, first_sums)
    g0, d0 = reduce_end(0)
    a0 = g0 / d0
    v[1] = y[0] - a0 * y[1]

    def second_sums():
        ret_copy(1).start()
        reduce_start(1, v[0] - a0 * y[0], v[1])

    product(2, second_sums)
    g1, d1 = reduce_end(1)
    b1 = g1 / g0
    a1 = g1 / (d1 - b1 * g1 / a0)

    def second(r0, w0, n0, n1):
        r1 = r0 - a0 * w0
        w1 = w0 - a0 * n0
        s1 = w1 + b1 * w0
        r2 = r1 - a1 * s1
        w2 = w1 - a1 * (n1 + b1 * n0)
        return r1, s1, r2, w2

    _, _, r2, w2 = second(v[0], y[0], y[1], y[2])
    reduce_start(2, r2, w2)
    ret_copy(2).start()

    def prepare(level, r0, w0, n0, n1):
        r1, s1, r2, w2 = second(r0, w0, n0, n1)
        p1 = r1 + b1 * r0
        x_out[0, level] = a0 * r0 + a1 * p1
        r_out[0, level] = r2
        tail[2, level] = p1
        tail[0, level] = s1
        tail[1, level] = w2

    def finish(level):
        r2 = r_out[0, level]
        x_out[0, level] = x_out[0, level] + a2 * (r2 + b2 * tail[2, level])
        r_out[0, level] = r2 - a2 * (tail[1, level] + b2 * tail[0, level])

    prepare(lev, v[0, lev], y[0, lev], y[1, lev], y[2, lev])
    locs[2].wait()
    for it in range(ITERS):
        ret_copy(it).wait_recv()
    prepare(other, home[...], rt[0], rt[1], rt[2])
    g2, d2 = reduce_end(2)
    b2 = g2 / g1
    a2 = g2 / (d2 - b2 * g2 / a1)

    finish(lev)
    finish(other)

    for s in swaps:
        s.wait_send()
    ob_copy.wait_send()
    pl.when(has_prev)(wn_copy.wait_send)
    for it in range(ITERS):
        edges_wait_send(eo, ei, h_send, h_recv, it)
        edges_wait_send(go, gi, g_send, g_recv, it)
        ret_copy(it).wait_send()
        most = red.at[it, pl.ds(0, count - 1)]
        pltpu.make_async_copy(most, most, rd_send.at[it]).wait()

        @pl.when(has_prev)
        def _():
            for k in range(many):
                back_copy(it, k).wait_send()

    @pl.when(has_next)
    def _():
        for k in range(many):
            forth_copy(ITERS - 1, k).wait_send()


def on_device(wins, tiles, right_side, error_weight, coeffs, obs_block, obs_pos, obs_weight):
    _, levels, rows, cols = right_side.shape
    nblk, width = obs_pos.shape[1:]
    f32 = jnp.float32
    vm = functools.partial(pltpu.VMEM, dtype=f32)
    dma = pltpu.SemaphoreType.DMA
    anyspace = pl.BlockSpec(memory_space=pltpu.HBM)
    vmem = pl.BlockSpec(memory_space=pltpu.VMEM)
    many = rows // EDGE
    scratch = [
        pltpu.VMEM(obs_block.shape, jnp.int32),
        pltpu.VMEM(obs_pos.shape, jnp.int32),
        vm(obs_weight.shape),
        vm((2, 2, rows, cols)),
        vm((ITERS, 2, rows, cols)),
        vm((2, rows, cols)),
        vm((rows, cols)),
        vm((4, 2, rows, cols)),
        vm((2, rows, cols)),
        vm((2, nblk + 8, width)),
        vm((2, rows, cols)),
        vm((ITERS, rows, cols)),
        vm((ITERS, rows, cols)),
        vm((rows, cols)),
        vm((ITERS, 2, 2, cols)),
        vm((ITERS, 2, 2, cols)),
        vm((ITERS, 2, 2, cols)),
        vm((ITERS, 2, 2, cols)),
        vm((ITERS, rows, cols)),
        vm((rows, cols)),
        vm((3, 2, rows, cols)),
        vm((ITERS, 2, 128)),
        vm((ITERS, wins * tiles, 2, 128)),
        dma((3 + many,)), dma((3 + many,)), dma((7,)),
        dma((ITERS, 2)), dma((ITERS, 2)),
        dma((2, ITERS, many)), dma((2, ITERS, many)),
        dma((ITERS, 2)), dma((ITERS, 2)),
        dma((ITERS,)), dma((ITERS,)),
        dma((ITERS,)), dma((ITERS,)),
        dma, dma,
        pltpu.SemaphoreType.REGULAR((1 + len(doubling(tiles)) + len(doubling(wins // 2)),)),
    ]
    out = vm(right_side.shape)
    return pl.pallas_call(
        functools.partial(kernel, wins, tiles),
        out_shape=(out, out),
        in_specs=[anyspace] * 6,
        out_specs=(vmem, vmem),
        scratch_shapes=scratch,
        compiler_params=pltpu.CompilerParams(has_side_effects=True, collective_id=0,
                                             vmem_limit_bytes=60 * 1024 * 1024),
    )(right_side, error_weight, coeffs, obs_block, obs_pos, obs_weight)


def solution(mesh):
    in_specs = (
        P("win", None, "tile", None),
        P("win", None, "tile", None),
        P(None, "win", None, "tile", None),
        P("win", "tile"),
        P("win", "tile", None),
        P("win", "tile", None),
    )
    out_specs = (P("win", None, "tile", None), P("win", None, "tile", None))
    return jax.shard_map(
        functools.partial(on_device, mesh.shape["win"], mesh.shape["tile"]),
        mesh=mesh, in_specs=in_specs, out_specs=out_specs, check_vma=False
    )
```

profile of v0, /device:TPU:0, one launch (start us, length us, event | category | flops | bytes accessed | tf_op | source)
XLA Modules:
  0.0 48.6 jit_solution(11514337511559388787)
XLA Ops:
  0.6 46.6 %shard_map.77 = (f32[1,2,32,1024]{3,2,1,0:T(8,128)S(1)}, f32[1,2,32,1024]{3,2,1,0:T(8,128)S(1)}) custom-call(f32[1,2,32,1024]{3,2,1,0:T(8,128)} %rhs.1, f32[1,2,32,1024]{3,2,1,0:T(8,128)} %err.1, f32[4,1,2,32,1024]{4,3,2,1,0:T(8,128)} %cof.1, s32[1,32]{1,0:T(1,128)} %oblk_in.1, s32[1,32,128]{2,1,0:T(8,128)} %opos_in.1, f32[1,32,128]{2,1,0:T(8,128)} %owgt_in.1), custom_call_target="tpu_custom_call" | custom-call | tf_op jit(solution)/shard_map/pallas_call | solution.py:494
  47.2 0.7 %copy.10 = f32[1,2,32,1024]{3,2,1,0:T(8,128)} copy(f32[1,2,32,1024]{3,2,1,0:T(8,128)S(1)} %get-tuple-element.2) | data formatting | bytes 524288
  47.9 0.7 %copy.11 = f32[1,2,32,1024]{3,2,1,0:T(8,128)} copy(f32[1,2,32,1024]{3,2,1,0:T(8,128)S(1)} %get-tuple-element.3) | data formatting | bytes 524288
where the time goes:
time: 48.8 us; the launch traced here: 48.6 us
  Pallas kernels  46.6 us (95%)
  local copies, waits for them, and re-layouts  1.41 us (3%)
  between operations  0.64 us (1%)
    pallas_call x1, Pallas kernels, on_device(): pl.pallas_call(functools.partial(kernel, wins, tiles), out_shape=(out, ou...  46.6 us
    unnamed x2, local copies, waits for them, and re-layouts  1.41 us

commit v1 on v0

v1 whole, which is shorter than its diff:
```python
import functools

import jax
import jax.numpy as jnp
from jax import lax
from jax.experimental import pallas as pl
from jax.experimental.pallas import tpu as pltpu
from jax.sharding import PartitionSpec as P

ITERS = 3
EDGE = 8
MOMENTS = 2 * ITERS - 1

HOP, BLOCK, SWAP_START, SWAP_FIELD, REDUCE = 2.1, 0.7, 2.0, 2.83, 5.2


def doubling(length):
    steps, known = [], 1
    while known < length - 1:
        steps.append(known)
        known *= 2
    return steps


class Steps:
    def __init__(self):
        self.todo = {}

    def add(self, name, needs, cost, run, sends=None, gets=None):
        self.todo[name] = (list(needs), cost, run, sends, gets)

    def order(self):
        senders = {sends[0]: name for name, (_, _, _, sends, _) in self.todo.items() if sends}
        after = {name: [] for name in self.todo}
        for name, (needs, _, _, _, gets) in self.todo.items():
            for need in needs:
                after[need].append((name, 0.0))
            if gets in senders:
                after[senders[gets]].append((name, self.todo[senders[gets]][3][2]))
        rank = {}

        def path(name):
            if name not in rank:
                rank[name] = self.todo[name][1] + max(
                    (wait + path(then) for then, wait in after[name]), default=0.0)
            return rank[name]

        for name in self.todo:
            path(name)
        now, done, arrive, free, result = 0.0, set(), {}, {}, []
        for _, (_, _, _, _, gets) in self.todo.items():
            if isinstance(gets, tuple) and gets[0] == "at":
                arrive[gets] = gets[1]
        left = dict(self.todo)
        while left:
            ready, soon = None, None
            for name, (needs, _, _, _, gets) in left.items():
                if any(need not in done for need in needs):
                    continue
                at = arrive.get(gets, None) if gets is not None else 0.0
                if at is None:
                    continue
                if at <= now:
                    if ready is None or rank[name] > rank[ready]:
                        ready = name
                elif soon is None or at < soon[0]:
                    soon = (at, name)
            pick = ready
            if pick is None:
                now, pick = soon
            _, cost, run, sends, _ = left.pop(pick)
            now += cost
            done.add(pick)
            if sends:
                message, link, latency, busy = sends
                begin = max(now, free.get(link, 0.0))
                free[link] = begin + busy
                arrive[message] = begin + busy + latency
            result.append((pick, run, now))
        return result


def two_sum(a, b):
    total = a + b
    back = total - a
    return total, (a - (total - back)) + (b - back)


def halves(a):
    big = 4097.0 * a
    high = big - (big - a)
    return high, a - high


def two_product(a, b):
    (ah, al), (bh, bl) = halves(a), halves(b)
    product = a * b
    return product, ((ah * bh - product) + ah * bl + al * bh) + al * bl


def pair_add(a, b):
    total, rest = two_sum(a[0], b[0])
    rest = rest + (a[1] + b[1])
    high = total + rest
    return high, rest - (high - total)


def pair_scale(a, factor):
    product, rest = two_product(a[0], factor)
    rest = rest + a[1] * factor
    high = product + rest
    return high, rest - (high - product)


def pair_rows(a, lo, hi):
    return a[0][lo:hi], a[1][lo:hi]


def pair_total(a):
    return jnp.sum(a[0], axis=1, keepdims=True) + jnp.sum(a[1], axis=1, keepdims=True)


def kernel(wins, tiles, rhs, err, cof, oblk_in, opos_in, owgt_in, x_out, r_out,
           obk, ops, owt, v, y, w, wn, c, d, ob, u, ui, vn, qb, qn, eo, ei, go, gi, rt, home,
           step, grad, early, late, reds, lasts,
           x_sem, xs_sem, l_sem, h_send, h_recv, b_send, b_recv, g_send, g_recv,
           rt_send, rt_recv, rd_send, rd_recv, wn_send, wn_recv, hello):
    me_w = lax.axis_index("win")
    me_t = lax.axis_index("tile")
    lev = lax.rem(me_w, 2)
    other = 1 - lev
    mate = me_w + 1 - 2 * lev
    has_next = me_w + 2 < wins
    has_prev = me_w >= 2
    has_north = me_t > 0
    has_south = me_t < tiles - 1
    rows, cols = v.shape[1], v.shape[2]
    count = wins * tiles
    me = me_w * tiles + me_t
    width = ops.shape[2]
    nblk = ops.shape[1]
    last = rows - 1
    blocks = rows // EDGE
    final = blocks - 1
    pieces = [0, final] + list(range(1, final))
    many = len(pieces)
    f32 = jnp.float32

    def rowset(k):
        return slice(k * EDGE, (k + 1) * EDGE)

    def remote(src, dst, ssem, rsem, win, tile):
        return pltpu.make_async_remote_copy(
            src_ref=src, dst_ref=dst, send_sem=ssem, recv_sem=rsem,
            device_id=(win, tile), device_id_type=pl.DeviceIdType.MESH)

    barrier = pltpu.get_barrier_semaphore()

    def signal(sem, win, tile):
        pl.semaphore_signal(sem, inc=1, device_id=(win, tile), device_id_type=pl.DeviceIdType.MESH)

    def greet(sem, ends):
        for there, win, tile in ends:
            pl.when(there)(functools.partial(signal, sem, win, tile))

    def met(sem, ends):
        pl.semaphore_wait(sem, sum(there.astype(jnp.int32) for there, _, _ in ends))

    def along_tile(hop):
        return [(me_t >= hop, me_w, me_t - hop), (me_t + hop < tiles, me_w, me_t + hop)]

    def along_win(hop):
        return [(me_w >= 2 * hop, me_w - 2 * hop, me_t),
                (me_w + 2 * hop < wins, me_w + 2 * hop, me_t)]

    facing = [(me_w >= 0, mate, me_t)]
    near = facing + along_tile(1) + along_win(1)
    rounds = ([along_tile(hop) for hop in doubling(tiles)] + [facing]
              + [along_win(hop) for hop in doubling(wins // 2)])

    greet(barrier, near)

    swaps = [
        remote(rhs.at[0, other], v.at[lev], xs_sem.at[0], x_sem.at[0], mate, me_t),
        remote(err.at[0, other], w.at[lev], xs_sem.at[1], x_sem.at[1], mate, me_t),
    ] + [
        remote(cof.at[:, 0, other, pl.ds(k * EDGE, EDGE)], c.at[:, lev, pl.ds(k * EDGE, EDGE)],
               xs_sem.at[3 + n], x_sem.at[3 + n], mate, me_t)
        for n, k in enumerate(pieces)
    ]
    arrivals = [
        remote(rhs.at[0, other], v.at[other], xs_sem.at[0], x_sem.at[0], mate, me_t),
        remote(err.at[0, other], w.at[other], xs_sem.at[1], x_sem.at[1], mate, me_t),
    ] + [
        remote(cof.at[:, 0, other, pl.ds(k * EDGE, EDGE)], c.at[:, other, pl.ds(k * EDGE, EDGE)],
               xs_sem.at[3 + n], x_sem.at[3 + n], mate, me_t)
        for n, k in enumerate(pieces)
    ]
    locs = {
        "block": pltpu.make_async_copy(oblk_in, obk, l_sem.at[4]),
        "pos": pltpu.make_async_copy(opos_in, ops, l_sem.at[5]),
        "weight": pltpu.make_async_copy(owgt_in, owt, l_sem.at[6]),
        "rhs": pltpu.make_async_copy(rhs.at[0, lev], v.at[lev], l_sem.at[0]),
        "err": pltpu.make_async_copy(err.at[0, lev], w.at[lev], l_sem.at[1]),
        "home": pltpu.make_async_copy(rhs.at[0, other], home, l_sem.at[2]),
        "cof": pltpu.make_async_copy(cof.at[:, 0, lev], c.at[:, lev], l_sem.at[3]),
    }
    for one in locs.values():
        one.start()
    met(barrier, near)
    for one in swaps[:3]:
        one.start()
    greet(hello.at[0], rounds[0])

    @pl.when(jnp.logical_not(has_north))
    def _():
        for it in range(ITERS):
            ei[it, 0] = jnp.zeros(ei.shape[2:], f32)
            gi[it, 0] = jnp.zeros(gi.shape[2:], f32)

    @pl.when(jnp.logical_not(has_south))
    def _():
        for it in range(ITERS):
            ei[it, 1] = jnp.zeros(ei.shape[2:], f32)
            gi[it, 1] = jnp.zeros(gi.shape[2:], f32)

    @pl.when(jnp.logical_not(has_prev))
    def _():
        for it in range(ITERS):
            ui[it] = jnp.zeros(ui.shape[1:], f32)

    @pl.when(jnp.logical_not(has_next))
    def _():
        wn[...] = jnp.zeros(wn.shape, f32)
        for it in range(ITERS):
            vn[it] = jnp.zeros(vn.shape[1:], f32)

    for one in ("block", "pos", "weight"):
        locs[one].wait()
    cell = lax.broadcasted_iota(jnp.int32, (width, width), 0)
    ones = jnp.ones((8, width), f32)
    ob[lev, nblk:, :] = jnp.zeros((8, width), f32)

    def per_block(b, carry):
        hit = jnp.where(cell == ops[0, pl.ds(b, 1), :], owt[0, pl.ds(b, 1), :], 0.0)
        total = lax.dot_general(ones, hit, (((1,), (1,)), ((), ())),
                                precision=lax.Precision.HIGHEST,
                                preferred_element_type=f32)
        ob[lev, pl.ds(b, 1), :] = total[0:1]
        return carry

    lax.fori_loop(0, nblk, per_block, 0)
    ob[lev, nblk:nblk + 1, 0:nblk] = obk[...].astype(f32)
    ob_copy = remote(ob.at[lev], ob.at[lev], xs_sem.at[2], x_sem.at[2], mate, me_t)
    ob_back = remote(ob.at[lev], ob.at[other], xs_sem.at[2], x_sem.at[2], mate, me_t)
    ob_copy.start()

    states = (v, y.at[0], y.at[1])
    row8 = lax.broadcasted_iota(jnp.int32, (EDGE, cols), 0)
    ways = (has_north, has_south)

    def east(a):
        return pltpu.roll(a, cols - 1, 1)

    def west(a):
        return pltpu.roll(a, 1, 1)

    def sides(a, top, bottom):
        return (jnp.where(row8 == 0, top, pltpu.roll(a, 1, 0))
                + jnp.where(row8 == EDGE - 1, bottom, pltpu.roll(a, EDGE - 1, 0)))

    def edge_copy(out, into, ssem, rsem, it, side):
        return remote(out.at[it, side], into.at[it, 1 - side], ssem.at[it, side],
                      rsem.at[it, 1 - side], me_w, me_t - 1 + 2 * side)

    def edge_in(out, into, ssem, rsem, it, side):
        return remote(out.at[it, 1 - side], into.at[it, side], ssem.at[it, 1 - side],
                      rsem.at[it, side], me_w, me_t - 1 + 2 * side)

    def back_copy(it, k):
        return remote(states[it].at[0, pl.ds(k * EDGE, EDGE)], vn.at[it, pl.ds(k * EDGE, EDGE)],
                      b_send.at[0, it, k], b_recv.at[0, it, k], me_w - 2, me_t)

    def forth_copy(it, k):
        return remote(u.at[it, 1, pl.ds(k * EDGE, EDGE)], ui.at[it, pl.ds(k * EDGE, EDGE)],
                      b_send.at[1, it, k], b_recv.at[1, it, k], me_w + 2, me_t)

    def ret_copy(it, k):
        return remote(y.at[it, other, pl.ds(k * EDGE, EDGE)], rt.at[it, pl.ds(k * EDGE, EDGE)],
                      rt_send.at[it, k], rt_recv.at[it, k], mate, me_t)

    wn_copy = remote(w.at[0], wn, wn_send, wn_recv, me_w - 2, me_t)

    def model(it, i, k):
        src = states[it]
        lo, hi = k * EDGE, (k + 1) * EDGE
        a = src[i, lo:hi]
        top = ei[it, 0, i:i + 1] if k == 0 else src[i, lo - 1:lo]
        bottom = ei[it, 1, i:i + 1] if k == final else src[i, hi:hi + 1]
        u[it, i, lo:hi] = (c[0, i, lo:hi] * a + c[1, i, lo:hi] * sides(a, top, bottom)
                           + c[2, i, lo:hi] * east(a) + c[3, i, lo:hi] * west(a))
        if i == 1:
            pl.when(has_next)(forth_copy(it, k).start)

    def misfit_here(it, k):
        at = rowset(k)
        qb[it, at] = w[1, at] * (states[it][1, at] - u[it, 0, at])

    def misfit_next(it, k):
        at = rowset(k)
        qn[it, at] = wn[at] * (vn[it, at] - u[it, 1, at])

    def adjoint(it, i, q, k, alone=None):
        lo, hi = k * EDGE, (k + 1) * EDGE
        a = q[it, lo:hi]
        if k == 0:
            top = gi[it, 0, i:i + 1]
        elif alone is not None:
            top = jnp.zeros((1, cols), f32)
        else:
            top = c[1, i, lo - 1:lo] * q[it, lo - 1:lo]
        if k == final:
            bottom = gi[it, 1, i:i + 1]
        elif alone is not None:
            bottom = jnp.zeros((1, cols), f32)
        else:
            bottom = c[1, i, hi:hi + 1] * q[it, hi:hi + 1]
        return (c[0, i, lo:hi] * a + sides(c[1, i, lo:hi] * a, top, bottom)
                + west(c[2, i, lo:hi] * a) + east(c[3, i, lo:hi] * a))

    def image(it, i, k, alone=None):
        at = rowset(k)
        src = states[it]
        if i == 1:
            return (qb[it, at] + d[1, at] * src[1, at]) - adjoint(it, 1, qn, k, alone)
        return (d[0, at] * src[0, at] - adjoint(it, 0, qb, k, alone)) + w[0, at] * (src[0, at] - ui[it, at])

    def diagonal():
        ob_back.wait_recv()
        per_row = cols // width
        base = lev * (rows * per_row)
        spot = lax.broadcasted_iota(jnp.int32, (rows, nblk), 0) * per_row + base
        for i in range(2):
            who = ob[i, nblk:nblk + 1, 0:nblk]
            sums = ob[i, 0:nblk, :]
            for k in range(per_row):
                hot = jnp.where((spot + k).astype(f32) == who, 1.0, 0.0)
                d[i, :, k * width:(k + 1) * width] = jnp.dot(
                    hot, sums, precision=lax.Precision.HIGHEST, preferred_element_type=f32)

    def lanes(a, b):
        total = None
        for k in range(blocks):
            at = rowset(k)
            here = a[0, at] * b[0, at] + a[1, at] * b[1, at]
            total = here if total is None else total + here
        total = jnp.sum(total, axis=0, keepdims=True)
        parts = [total[:, k * width:(k + 1) * width] for k in range(cols // width)]
        while len(parts) > 1:
            parts = [sum(parts[k:k + 2]) for k in range(0, len(parts), 2)]
        return parts[0]

    def to_all(part, into, sems):
        def send(o, carry):
            to = lax.rem(me + o, count)
            remote(part, into.at[me], rd_send.at[sems], rd_recv.at[sems],
                   to // tiles, lax.rem(to, tiles)).start()
            return carry

        lax.fori_loop(1, count, send, 0)
        into[me] = part[...]

    def from_all(into, sems):
        most = into.at[pl.ds(0, count - 1)]
        pltpu.make_async_copy(most, most, rd_recv.at[sems]).wait()
        high, low = into[0], jnp.zeros(into.shape[1:], f32)
        for k in range(1, count):
            high, rest = two_sum(high, into[k])
            low = low + rest
        return high, low

    S = Steps()
    scalars = {}

    def spread(at):
        met(hello.at[at], rounds[at])
        if at + 1 < len(rounds):
            greet(hello.at[at + 1], rounds[at + 1])

    for n in range(len(rounds)):
        S.add(("spread", n), [("spread", n - 1)] if n else [], 0.05, functools.partial(spread, n),
              sends=(("hello", n), "hello", 2.5, 0.0), gets=("hello", n - 1) if n else ("at", 1.5))
    met_all = [("spread", len(rounds) - 1)]

    S.add("rhs here", [], 0.0, locs["rhs"].wait, gets=("at", 0.5))
    S.add("err here", [], 0.0, locs["err"].wait, gets=("at", 0.5))
    S.add("cof here", [], 0.0, locs["cof"].wait, gets=("at", 1.0))
    S.add("home", [], 0.0, locs["home"].wait, gets=("at", 9.0))
    S.add("rhs there", [], 0.01, arrivals[0].wait_recv, gets=("at", SWAP_START + SWAP_FIELD))

    def err_there():
        arrivals[1].wait_recv()
        swaps[3].start()
        pl.when(has_prev)(wn_copy.start)

    S.add("err there", ["err here"], 0.03, err_there, sends=("next weights", "weights", 4.8, 0.0),
          gets=("at", SWAP_START + 2 * SWAP_FIELD))
    S.add("next weights", [], 0.01, lambda: pl.when(has_next)(wn_copy.wait_recv), gets="next weights")
    S.add("diagonal", [], 0.6, diagonal, gets=("at", SWAP_START + 1.3 * SWAP_FIELD))

    def piece(n):
        arrivals[2 + n].wait_recv()
        if 4 + n < len(swaps):
            swaps[4 + n].start()

    for n, k in enumerate(pieces):
        S.add(("cof", k), ["cof here"], 0.02, functools.partial(piece, n),
              gets=("at", SWAP_START + SWAP_FIELD * (2 + 4.0 * (n + 1) / many)))

    def whole_rows(it, i, k):
        if it == 0:
            return ["rhs here", "rhs there"]
        return [("image", it - 1, i, k)]

    def edges_out(it, side):
        k, at = (0, 0) if side == 0 else (final, last)
        if it == 1:
            at = 0 if side == 0 else EDGE - 1
            for i in range(2):
                eo[it, side, i:i + 1] = image(0, i, k, alone=True)[at:at + 1]
        else:
            for i in range(2):
                eo[it, side, i:i + 1] = states[it][i, at:at + 1]
        pl.when(ways[side])(edge_copy(eo, ei, h_send, h_recv, it, side).start)

    def adjoint_out(it, side):
        at = 0 if side == 0 else last
        here = slice(at, at + 1)
        go[it, side, 0:1] = c[1, 0, here] * qb[it, here]
        go[it, side, 1:2] = c[1, 1, here] * qn[it, here]
        pl.when(ways[side])(edge_copy(go, gi, g_send, g_recv, it, side).start)

    def store_image(it, i, k):
        y[it, i, rowset(k)] = image(it, i, k)
        if i == 0 and it + 1 < ITERS:
            pl.when(has_prev)(back_copy(it + 1, k).start)

    for it in range(ITERS):
        for side, k in ((0, 0), (1, final)):
            if it == 1:
                needs = [("here", 0, k), ("next", 0, k), ("forth", 0, k), ("adjoint in", 0, side), "diagonal"]
            else:
                needs = whole_rows(it, 0, k) + whole_rows(it, 1, k)
            S.add(("edges out", it, side), needs, 0.12, functools.partial(edges_out, it, side),
                  sends=(("edges", it, side), ("tile", side), HOP, 0.1))
            S.add(("edges in", it, side), [], 0.02, lambda it=it, side=side: pl.when(ways[side])(
                edge_in(eo, ei, h_send, h_recv, it, side).wait_recv), gets=("edges", it, 1 - side))
            S.add(("adjoint out", it, side), [("here", it, k), ("next", it, k)], 0.06,
                  functools.partial(adjoint_out, it, side),
                  sends=(("adjoint", it, side), ("tile", side), HOP, 0.1))
            S.add(("adjoint in", it, side), [], 0.02, lambda it=it, side=side: pl.when(ways[side])(
                edge_in(go, gi, g_send, g_recv, it, side).wait_recv), gets=("adjoint", it, 1 - side))
        for k in range(blocks):
            if it == 0:
                S.add(("back out", 0, k), whole_rows(0, 0, k), 0.02,
                      lambda k=k: pl.when(has_prev)(back_copy(0, k).start),
                      sends=(("back", 0, k), "back", HOP, BLOCK))
            S.add(("back", it, k), [], 0.02, lambda it=it, k=k: pl.when(has_next)(
                back_copy(it, k).wait_recv), gets=("back", it, k))
            S.add(("forth", it, k), [], 0.02, lambda it=it, k=k: pl.when(has_prev)(
                forth_copy(it, k).wait_recv), gets=("forth", it, k))
            around = [m for m in (k - 1, k, k + 1) if 0 <= m < blocks]
            ends = [side for side, m in ((0, 0), (1, final)) if m == k]
            for i in range(2):
                needs = [("cof", k)] + [("edges in", it, side) for side in ends]
                for m in around:
                    needs += whole_rows(it, i, m)
                S.add(("model", it, i, k), needs, 0.05, functools.partial(model, it, i, k),
                      sends=(("forth", it, k), "forth", HOP, BLOCK) if i == 1 else None)
                needs = ["diagonal", "err here", "err there"] + [("adjoint in", it, side) for side in ends]
                needs += [("next" if i else "here", it, m) for m in around]
                needs += [("here", it, k)] if i else [("forth", it, k)]
                S.add(("image", it, i, k), needs, 0.06, functools.partial(store_image, it, i, k),
                      sends=(("back", it + 1, k), "back", HOP, BLOCK) if i == 0 and it + 1 < ITERS else None)
            S.add(("here", it, k), ["err here", "err there", ("model", it, 0, k)], 0.03,
                  functools.partial(misfit_here, it, k))
            S.add(("next", it, k), ["next weights", ("model", it, 1, k), ("back", it, k)], 0.03,
                  functools.partial(misfit_next, it, k))
            S.add(("ret out", it, k), [("image", it, 0, k), ("image", it, 1, k)], 0.02,
                  lambda it=it, k=k: ret_copy(it, k).start(),
                  sends=(("ret", it, k), "ret", HOP, BLOCK))
            S.add(("ret", it, k), [], 0.01, lambda it=it, k=k: ret_copy(it, k).wait_recv(),
                  gets=("ret", it, k))

    def images(it):
        return [("image", it, i, k) for i in range(2) for k in range(blocks)]

    def moment(n, a, b):
        early[n:n + 1] = lanes(a, b)

    S.add("moment 0", ["rhs here", "rhs there"], 0.15, lambda: moment(0, v, v))
    S.add("moment 1", images(0), 0.3, lambda: (moment(1, v, y.at[0]), moment(2, y.at[0], y.at[0])))
    S.add("moment 3", images(1), 0.3,
          lambda: (moment(3, y.at[0], y.at[1]), moment(4, y.at[1], y.at[1])))

    S.add("early out", ["moment 0", "moment 1", "moment 3"] + met_all, 0.4,
          lambda: to_all(early, reds, 0), sends=("early", "all", REDUCE, 0.0))

    def late_out():
        late[...] = lanes(y.at[1], y.at[2])
        to_all(late, lasts, 1)

    S.add("late out", images(2) + met_all, 0.5, late_out, sends=("late", "all", REDUCE, 0.0))

    def early_in():
        m = from_all(reds, 0)
        plain = jnp.sum(m[0], axis=1, keepdims=True)
        g0 = plain[0:1]
        a0 = g0 / plain[1:2]
        less = pair_add(pair_rows(m, 0, 4), pair_scale(pair_rows(m, 1, 5), -a0))
        less = pair_add(pair_rows(less, 0, 3), pair_scale(pair_rows(less, 1, 4), -a0))
        one = pair_total(less)
        g1, d1 = one[0:1], one[1:2]
        b1 = g1 / g0
        a1 = g1 / (d1 - b1 * g1 / a0)
        p1 = -(a0 + a1 + a1 * b1)
        p2 = a0 * a1
        q = pair_add(pair_add(pair_rows(m, 0, 3), pair_scale(pair_rows(m, 1, 4), p1)),
                     pair_scale(pair_rows(m, 2, 5), p2))
        g2 = pair_total(pair_add(pair_add(pair_rows(q, 0, 1), pair_scale(pair_rows(q, 1, 2), p1)),
                                 pair_scale(pair_rows(q, 2, 3), p2)))
        rest = pair_add(pair_rows(m, 3, 4), pair_scale(pair_rows(m, 4, 5), p1))
        base = pair_add(pair_add(pair_rows(q, 1, 2), pair_scale(pair_rows(q, 2, 3), p1)),
                        pair_scale(rest, p2))
        scalars.update(a0=a0, a1=a1, b1=b1, p1=p1, p2=p2, g2=g2, b2=g2 / g1, base=base)

    S.add("early in", [], 0.6, early_in, gets="early")

    def late_in():
        s = scalars
        m = from_all(lasts, 1)
        d2 = pair_total(pair_add(s["base"], pair_scale(pair_scale(m, s["p2"]), s["p2"])))
        scalars["a2"] = s["g2"] / (d2 - s["b2"] * s["g2"] / s["a1"])

    S.add("late in", ["early in"], 0.4, late_in, gets="late")

    def own(level):
        return lambda at: v[level, at], lambda it, at: y[it, level, at]

    def away():
        return lambda at: home[at], lambda it, at: rt[it, at]

    def solve(level, source, k):
        s = scalars
        at = rowset(k)
        first, images_of = source
        r0, y0, y1 = first(at), images_of(0, at), images_of(1, at)
        p = (r0 - s["a0"] * y0) + s["b1"] * r0
        r2 = (r0 + s["p1"] * y0) + s["p2"] * y1
        x_out[0, level, at] = s["a0"] * r0 + s["a1"] * p
        r_out[0, level, at] = r2
        step[level, at] = r2 + s["b2"] * p

    def tail(level, source, k):
        s = scalars
        at = rowset(k)
        _, images_of = source
        y0, y1, y2 = images_of(0, at), images_of(1, at), images_of(2, at)
        s1 = (y0 - s["a0"] * y1) + s["b1"] * y0
        grad[level, at] = ((y0 + s["p1"] * y1) + s["p2"] * y2) + s["b2"] * s1

    def finish(level, k):
        at = rowset(k)
        x_out[0, level, at] = x_out[0, level, at] + scalars["a2"] * step[level, at]
        r_out[0, level, at] = r_out[0, level, at] - scalars["a2"] * grad[level, at]

    for k in range(blocks):
        S.add(("solve own", k), ["early in"] + [("image", it, i, k) for it in range(2) for i in range(2)],
              0.06, functools.partial(solve, lev, own(lev), k))
        S.add(("solve away", k), ["early in", "home"] + [("ret", it, k) for it in range(2)],
              0.06, functools.partial(solve, other, away(), k))
        S.add(("tail own", k), ["early in"] + [("image", it, i, k) for it in range(3) for i in range(2)],
              0.06, functools.partial(tail, lev, own(lev), k))
        S.add(("tail away", k), ["early in"] + [("ret", it, k) for it in range(3)],
              0.06, functools.partial(tail, other, away(), k))
        S.add(("finish own", k), ["late in", ("solve own", k), ("tail own", k)],
              0.04, functools.partial(finish, lev, k))
        S.add(("finish away", k), ["late in", ("solve away", k), ("tail away", k)],
              0.04, functools.partial(finish, other, k))

    order = S.order()
    if SHOW:
        for name, _, when in order:
            print(f"{when:6.2f}", name)
    for name, run, _ in order:
        run()

    for one in swaps:
        one.wait_send()
    ob_copy.wait_send()
    pl.when(has_prev)(wn_copy.wait_send)
    for it in range(ITERS):
        for side in range(2):
            pl.when(ways[side])(edge_copy(eo, ei, h_send, h_recv, it, side).wait_send)
            pl.when(ways[side])(edge_copy(go, gi, g_send, g_recv, it, side).wait_send)
        for k in range(blocks):
            ret_copy(it, k).wait_send()

        @pl.when(has_prev)
        def _():
            for k in range(blocks):
                back_copy(it, k).wait_send()

        @pl.when(has_next)
        def _():
            for k in range(blocks):
                forth_copy(it, k).wait_send()

    for sems, into in ((0, reds), (1, lasts)):
        most = into.at[pl.ds(0, count - 1)]
        pltpu.make_async_copy(most, most, rd_send.at[sems]).wait()


SHOW = False


def on_device(wins, tiles, right_side, error_weight, coeffs, obs_block, obs_pos, obs_weight):
    _, levels, rows, cols = right_side.shape
    nblk, width = obs_pos.shape[1:]
    f32 = jnp.float32
    vm = functools.partial(pltpu.VMEM, dtype=f32)
    dma = pltpu.SemaphoreType.DMA
    hbm = pl.BlockSpec(memory_space=pltpu.HBM)
    vmem = pl.BlockSpec(memory_space=pltpu.VMEM)
    blocks = rows // EDGE
    field = (rows, cols)
    edge = vm((ITERS, 2, 2, cols))
    scratch = [
        pltpu.VMEM(obs_block.shape, jnp.int32),
        pltpu.VMEM(obs_pos.shape, jnp.int32),
        vm(obs_weight.shape),
        vm((2,) + field),
        vm((ITERS, 2) + field),
        vm((2,) + field),
        vm(field),
        vm((4, 2) + field),
        vm((2,) + field),
        vm((2, nblk + 8, width)),
        vm((ITERS, 2) + field),
        vm((ITERS,) + field),
        vm((ITERS,) + field),
        vm((ITERS,) + field),
        vm((ITERS,) + field),
        edge, edge, edge, edge,
        vm((ITERS,) + field),
        vm(field),
        vm((2,) + field),
        vm((2,) + field),
        vm((MOMENTS, width)),
        vm((1, width)),
        vm((wins * tiles, MOMENTS, width)),
        vm((wins * tiles, 1, width)),
        dma((3 + blocks,)), dma((3 + blocks,)), dma((7,)),
        dma((ITERS, 2)), dma((ITERS, 2)),
        dma((2, ITERS, blocks)), dma((2, ITERS, blocks)),
        dma((ITERS, 2)), dma((ITERS, 2)),
        dma((ITERS, blocks)), dma((ITERS, blocks)),
        dma((2,)), dma((2,)),
        dma, dma,
        pltpu.SemaphoreType.REGULAR((1 + len(doubling(tiles)) + len(doubling(wins // 2)),)),
    ]
    out = vm(right_side.shape)
    return pl.pallas_call(
        functools.partial(kernel, wins, tiles),
        out_shape=(out, out),
        in_specs=[hbm] * 6,
        out_specs=(vmem, vmem),
        scratch_shapes=scratch,
        compiler_params=pltpu.CompilerParams(has_side_effects=True, collective_id=0,
                                             vmem_limit_bytes=60 * 1024 * 1024),
    )(right_side, error_weight, coeffs, obs_block, obs_pos, obs_weight)


def solution(mesh):
    in_specs = (
        P("win", None, "tile", None),
        P("win", None, "tile", None),
        P(None, "win", None, "tile", None),
        P("win", "tile"),
        P("win", "tile", None),
        P("win", "tile", None),
    )
    out_specs = (P("win", None, "tile", None), P("win", None, "tile", None))
    return jax.shard_map(
        functools.partial(on_device, mesh.shape["win"], mesh.shape["tile"]),
        mesh=mesh, in_specs=in_specs, out_specs=out_specs, check_vma=False
    )
```

time: 48.8 us -> 46.2 us (0.947)
  Pallas kernels: 46.6 us -> 44 us
    pallas_call x1, Pallas kernels: 46.6 us -> 44 us  [on_device(): pl.pallas_call(functools.partial(kernel, wins, tiles), out_shape=(out, ou...]
where the time goes in v1:
time: 46.2 us; the launch traced here: 46 us
  Pallas kernels  44 us (95%)
  local copies, waits for them, and re-layouts  1.41 us (3%)
  between operations  0.64 us (1%)
    pallas_call x1, Pallas kernels, on_device(): pl.pallas_call(functools.partial(kernel, wins, tiles), out_shape=(out, ou...  44 us
    unnamed x2, local copies, waits for them, and re-layouts  1.41 us

profile of v1, /device:TPU:0, one launch (start us, length us, event | category | flops | bytes accessed | tf_op | source)
XLA Modules:
  0.0 46.0 jit_solution(17415343235895133569)
XLA Ops:
  0.6 44.0 %shard_map.77 = (f32[1,2,32,1024]{3,2,1,0:T(8,128)S(1)}, f32[1,2,32,1024]{3,2,1,0:T(8,128)S(1)}) custom-call(f32[1,2,32,1024]{3,2,1,0:T(8,128)} %rhs.1, f32[1,2,32,1024]{3,2,1,0:T(8,128)} %err.1, f32[4,1,2,32,1024]{4,3,2,1,0:T(8,128)} %cof.1, s32[1,32]{1,0:T(1,128)} %oblk_in.1, s32[1,32,128]{2,1,0:T(8,128)} %opos_in.1, f32[1,32,128]{2,1,0:T(8,128)} %owgt_in.1), custom_call_target="tpu_custom_call" | custom-call | tf_op jit(solution)/shard_map/pallas_call | solution.py:673
  44.6 0.7 %copy.10 = f32[1,2,32,1024]{3,2,1,0:T(8,128)} copy(f32[1,2,32,1024]{3,2,1,0:T(8,128)S(1)} %get-tuple-element.2) | data formatting | bytes 524288
  45.3 0.7 %copy.11 = f32[1,2,32,1024]{3,2,1,0:T(8,128)} copy(f32[1,2,32,1024]{3,2,1,0:T(8,128)S(1)} %get-tuple-element.3) | data formatting | bytes 524288

commit v2 on v1

--- a/solution.py
+++ b/solution.py
@@ -11,7 +11,7 @@
 EDGE = 8
 MOMENTS = 2 * ITERS - 1
 
-HOP, BLOCK, SWAP_START, SWAP_FIELD, REDUCE = 2.1, 0.7, 2.0, 2.83, 5.2
+HOP, TILE_HOPS, BLOCK, SWAP_START, SWAP_FIELD, REDUCE, BEGIN = 2.2, (2.8, 1.5), 0.7, 2.2, 2.83, 5.2, 7.5
 
 
 def doubling(length):
@@ -47,7 +47,7 @@
 
         for name in self.todo:
             path(name)
-        now, done, arrive, free, result = 0.0, set(), {}, {}, []
+        now, done, arrive, free, result = BEGIN, set(), {}, {}, []
         for _, (_, _, _, _, gets) in self.todo.items():
             if isinstance(gets, tuple) and gets[0] == "at":
                 arrive[gets] = gets[1]
@@ -122,7 +122,7 @@
 
 def kernel(wins, tiles, rhs, err, cof, oblk_in, opos_in, owgt_in, x_out, r_out,
            obk, ops, owt, v, y, w, wn, c, d, ob, u, ui, vn, qb, qn, eo, ei, go, gi, rt, home,
-           step, grad, early, late, reds, lasts,
+           step, grad, energy, early, late, reds, lasts,
            x_sem, xs_sem, l_sem, h_send, h_recv, b_send, b_recv, g_send, g_recv,
            rt_send, rt_recv, rd_send, rd_recv, wn_send, wn_recv, hello):
     me_w = lax.axis_index("win")
@@ -132,8 +132,6 @@
     mate = me_w + 1 - 2 * lev
     has_next = me_w + 2 < wins
     has_prev = me_w >= 2
-    has_north = me_t > 0
-    has_south = me_t < tiles - 1
     rows, cols = v.shape[1], v.shape[2]
     count = wins * tiles
     me = me_w * tiles + me_t
@@ -142,12 +140,27 @@
     last = rows - 1
     blocks = rows // EDGE
     final = blocks - 1
-    pieces = [0, final] + list(range(1, final))
+    pieces = list(range(final - 1)) + [final, final - 1]
     many = len(pieces)
     f32 = jnp.float32
 
+    odd = lax.rem(me_t, 2)
+    even = odd == 0
+
+    def first_row(k):
+        return pl.multiple_of((k + odd * (final - 2 * k)) * EDGE, EDGE)
+
     def rowset(k):
-        return slice(k * EDGE, (k + 1) * EDGE)
+        return pl.ds(first_row(k), EDGE)
+
+    def row_beyond(k, side):
+        return pl.ds(first_row(k) - 1 + 9 * odd if side == 0 else first_row(k) + EDGE - 9 * odd, 1)
+
+    def edge_row(side):
+        return pl.ds(odd * last if side == 0 else last - odd * last, 1)
+
+    beside = (me_t - 1 + 2 * odd, me_t + 1 - 2 * odd)
+    ways = tuple(jnp.logical_and(tile >= 0, tile < tiles) for tile in beside)
 
     def remote(src, dst, ssem, rsem, win, tile):
         return pltpu.make_async_remote_copy(
@@ -184,7 +197,7 @@
         remote(rhs.at[0, other], v.at[lev], xs_sem.at[0], x_sem.at[0], mate, me_t),
         remote(err.at[0, other], w.at[lev], xs_sem.at[1], x_sem.at[1], mate, me_t),
     ] + [
-        remote(cof.at[:, 0, other, pl.ds(k * EDGE, EDGE)], c.at[:, lev, pl.ds(k * EDGE, EDGE)],
+        remote(cof.at[:, 0, other, rowset(k)], c.at[:, lev, rowset(k)],
                xs_sem.at[3 + n], x_sem.at[3 + n], mate, me_t)
         for n, k in enumerate(pieces)
     ]
@@ -192,7 +205,7 @@
         remote(rhs.at[0, other], v.at[other], xs_sem.at[0], x_sem.at[0], mate, me_t),
         remote(err.at[0, other], w.at[other], xs_sem.at[1], x_sem.at[1], mate, me_t),
     ] + [
-        remote(cof.at[:, 0, other, pl.ds(k * EDGE, EDGE)], c.at[:, other, pl.ds(k * EDGE, EDGE)],
+        remote(cof.at[:, 0, other, rowset(k)], c.at[:, other, rowset(k)],
                xs_sem.at[3 + n], x_sem.at[3 + n], mate, me_t)
         for n, k in enumerate(pieces)
     ]
@@ -212,17 +225,12 @@
         one.start()
     greet(hello.at[0], rounds[0])
 
-    @pl.when(jnp.logical_not(has_north))
-    def _():
-        for it in range(ITERS):
-            ei[it, 0] = jnp.zeros(ei.shape[2:], f32)
-            gi[it, 0] = jnp.zeros(gi.shape[2:], f32)
-
-    @pl.when(jnp.logical_not(has_south))
-    def _():
-        for it in range(ITERS):
-            ei[it, 1] = jnp.zeros(ei.shape[2:], f32)
-            gi[it, 1] = jnp.zeros(gi.shape[2:], f32)
+    for side in range(2):
+        @pl.when(jnp.logical_not(ways[side]))
+        def _():
+            for it in range(ITERS):
+                ei[it, side] = jnp.zeros(ei.shape[2:], f32)
+                gi[it, side] = jnp.zeros(gi.shape[2:], f32)
 
     @pl.when(jnp.logical_not(has_prev))
     def _():
@@ -235,29 +243,8 @@
         for it in range(ITERS):
             vn[it] = jnp.zeros(vn.shape[1:], f32)
 
-    for one in ("block", "pos", "weight"):
-        locs[one].wait()
-    cell = lax.broadcasted_iota(jnp.int32, (width, width), 0)
-    ones = jnp.ones((8, width), f32)
-    ob[lev, nblk:, :] = jnp.zeros((8, width), f32)
-
-    def per_block(b, carry):
-        hit = jnp.where(cell == ops[0, pl.ds(b, 1), :], owt[0, pl.ds(b, 1), :], 0.0)
-        total = lax.dot_general(ones, hit, (((1,), (1,)), ((), ())),
-                                precision=lax.Precision.HIGHEST,
-                                preferred_element_type=f32)
-        ob[lev, pl.ds(b, 1), :] = total[0:1]
-        return carry
-
-    lax.fori_loop(0, nblk, per_block, 0)
-    ob[lev, nblk:nblk + 1, 0:nblk] = obk[...].astype(f32)
-    ob_copy = remote(ob.at[lev], ob.at[lev], xs_sem.at[2], x_sem.at[2], mate, me_t)
-    ob_back = remote(ob.at[lev], ob.at[other], xs_sem.at[2], x_sem.at[2], mate, me_t)
-    ob_copy.start()
-
     states = (v, y.at[0], y.at[1])
     row8 = lax.broadcasted_iota(jnp.int32, (EDGE, cols), 0)
-    ways = (has_north, has_south)
 
     def east(a):
         return pltpu.roll(a, cols - 1, 1)
@@ -265,40 +252,39 @@
     def west(a):
         return pltpu.roll(a, 1, 1)
 
-    def sides(a, top, bottom):
+    def sides(a, beyond):
+        top, bottom = jnp.where(even, beyond[0], beyond[1]), jnp.where(even, beyond[1], beyond[0])
         return (jnp.where(row8 == 0, top, pltpu.roll(a, 1, 0))
                 + jnp.where(row8 == EDGE - 1, bottom, pltpu.roll(a, EDGE - 1, 0)))
 
-    def edge_copy(out, into, ssem, rsem, it, side):
-        return remote(out.at[it, side], into.at[it, 1 - side], ssem.at[it, side],
-                      rsem.at[it, 1 - side], me_w, me_t - 1 + 2 * side)
-
-    def edge_in(out, into, ssem, rsem, it, side):
-        return remote(out.at[it, 1 - side], into.at[it, side], ssem.at[it, 1 - side],
-                      rsem.at[it, side], me_w, me_t - 1 + 2 * side)
+    def edge_copy(out, into, ssem, rsem, it, side, i):
+        return remote(out.at[it, side, i], into.at[it, side, i], ssem.at[it, side, i],
+                      rsem.at[it, side, i], me_w, beside[side])
 
     def back_copy(it, k):
-        return remote(states[it].at[0, pl.ds(k * EDGE, EDGE)], vn.at[it, pl.ds(k * EDGE, EDGE)],
+        return remote(states[it].at[0, rowset(k)], vn.at[it, rowset(k)],
                       b_send.at[0, it, k], b_recv.at[0, it, k], me_w - 2, me_t)
 
     def forth_copy(it, k):
-        return remote(u.at[it, 1, pl.ds(k * EDGE, EDGE)], ui.at[it, pl.ds(k * EDGE, EDGE)],
+        return remote(u.at[it, 1, rowset(k)], ui.at[it, rowset(k)],
                       b_send.at[1, it, k], b_recv.at[1, it, k], me_w + 2, me_t)
 
     def ret_copy(it, k):
-        return remote(y.at[it, other, pl.ds(k * EDGE, EDGE)], rt.at[it, pl.ds(k * EDGE, EDGE)],
+        return remote(y.at[it, other, rowset(k)], rt.at[it, rowset(k)],
                       rt_send.at[it, k], rt_recv.at[it, k], mate, me_t)
 
     wn_copy = remote(w.at[0], wn, wn_send, wn_recv, me_w - 2, me_t)
 
+    def end_side(k):
+        return 0 if k == 0 else 1 if k == final else None
+
     def model(it, i, k):
-        src = states[it]
-        lo, hi = k * EDGE, (k + 1) * EDGE
-        a = src[i, lo:hi]
-        top = ei[it, 0, i:i + 1] if k == 0 else src[i, lo - 1:lo]
-        bottom = ei[it, 1, i:i + 1] if k == final else src[i, hi:hi + 1]
-        u[it, i, lo:hi] = (c[0, i, lo:hi] * a + c[1, i, lo:hi] * sides(a, top, bottom)
-                           + c[2, i, lo:hi] * east(a) + c[3, i, lo:hi] * west(a))
+        src, at = states[it], rowset(k)
+        a = src[i, at]
+        beyond = [ei[it, side, i] if side == end_side(k) else src[i, row_beyond(k, side)]
+                  for side in range(2)]
+        u[it, i, at] = (c[0, i, at] * a + c[1, i, at] * sides(a, beyond)
+                        + c[2, i, at] * east(a) + c[3, i, at] * west(a))
         if i == 1:
             pl.when(has_next)(forth_copy(it, k).start)
 
@@ -311,22 +297,19 @@
         qn[it, at] = wn[at] * (vn[it, at] - u[it, 1, at])
 
     def adjoint(it, i, q, k, alone=None):
-        lo, hi = k * EDGE, (k + 1) * EDGE
-        a = q[it, lo:hi]
-        if k == 0:
-            top = gi[it, 0, i:i + 1]
-        elif alone is not None:
-            top = jnp.zeros((1, cols), f32)
-        else:
-            top = c[1, i, lo - 1:lo] * q[it, lo - 1:lo]
-        if k == final:
-            bottom = gi[it, 1, i:i + 1]
-        elif alone is not None:
-            bottom = jnp.zeros((1, cols), f32)
-        else:
-            bottom = c[1, i, hi:hi + 1] * q[it, hi:hi + 1]
-        return (c[0, i, lo:hi] * a + sides(c[1, i, lo:hi] * a, top, bottom)
-                + west(c[2, i, lo:hi] * a) + east(c[3, i, lo:hi] * a))
+        at = rowset(k)
+        a = q[it, at]
+        beyond = []
+        for side in range(2):
+            if side == end_side(k):
+                beyond.append(gi[it, side, i])
+            elif alone is not None:
+                beyond.append(jnp.zeros((1, cols), f32))
+            else:
+                row = row_beyond(k, side)
+                beyond.append(c[1, i, row] * q[it, row])
+        return (c[0, i, at] * a + sides(c[1, i, at] * a, beyond)
+                + west(c[2, i, at] * a) + east(c[3, i, at] * a))
 
     def image(it, i, k, alone=None):
         at = rowset(k)
@@ -351,9 +334,12 @@
     def lanes(a, b):
         total = None
         for k in range(blocks):
-            at = rowset(k)
+            at = slice(k * EDGE, (k + 1) * EDGE)
             here = a[0, at] * b[0, at] + a[1, at] * b[1, at]
             total = here if total is None else total + here
+        return folded(total)
+
+    def folded(total):
         total = jnp.sum(total, axis=0, keepdims=True)
         parts = [total[:, k * width:(k + 1) * width] for k in range(cols // width)]
         while len(parts) > 1:
@@ -361,8 +347,10 @@
         return parts[0]
 
     def to_all(part, into, sems):
+        turned = 2 * me < count
+
         def send(o, carry):
-            to = lax.rem(me + o, count)
+            to = lax.rem(me + jnp.where(turned, count - o, o), count)
             remote(part, into.at[me], rd_send.at[sems], rd_recv.at[sems],
                    to // tiles, lax.rem(to, tiles)).start()
             return carry
@@ -379,6 +367,47 @@
             low = low + rest
         return high, low
 
+    def edges_out(it, side, i):
+        if it == 0:
+            eo[it, side, i] = v[i, edge_row(side)]
+        else:
+            whole = image(it - 1, i, 0 if side == 0 else final, alone=True)
+            low, high = whole[0:1], whole[EDGE - 1:EDGE]
+            eo[it, side, i] = jnp.where(even, low, high) if side == 0 else jnp.where(even, high, low)
+        pl.when(ways[side])(edge_copy(eo, ei, h_send, h_recv, it, side, i).start)
+
+    for one in ("block", "pos", "weight"):
+        locs[one].wait()
+    cell = lax.broadcasted_iota(jnp.int32, (width, width), 0)
+    ones = jnp.ones((8, width), f32)
+    ob[lev, nblk:, :] = jnp.zeros((8, width), f32)
+
+    def per_block(b, carry):
+        hit = jnp.where(cell == ops[0, pl.ds(b, 1), :], owt[0, pl.ds(b, 1), :], 0.0)
+        total = lax.dot_general(ones, hit, (((1,), (1,)), ((), ())),
+                                precision=lax.Precision.HIGHEST,
+                                preferred_element_type=f32)
+        ob[lev, pl.ds(b, 1), :] = total[0:1]
+        return carry
+
+    most = nblk - nblk // 4
+    lax.fori_loop(0, most, per_block, 0)
+    locs["rhs"].wait()
+    arrivals[0].wait_recv()
+    swaps[3].start()
+    for k in range(blocks):
+        pl.when(has_prev)(back_copy(0, k).start)
+    for side in range(2):
+        for i in range(2):
+            edges_out(0, side, i)
+    lax.fori_loop(most, nblk, per_block, 0)
+    ob[lev, nblk:nblk + 1, 0:nblk] = obk[...].astype(f32)
+    ob_copy = remote(ob.at[lev], ob.at[lev], xs_sem.at[2], x_sem.at[2], mate, me_t)
+    ob_back = remote(ob.at[lev], ob.at[other], xs_sem.at[2], x_sem.at[2], mate, me_t)
+    ob_copy.start()
+    for one in swaps[4:]:
+        one.start()
+
     S = Steps()
     scalars = {}
 
@@ -389,56 +418,38 @@
 
     for n in range(len(rounds)):
         S.add(("spread", n), [("spread", n - 1)] if n else [], 0.05, functools.partial(spread, n),
-              sends=(("hello", n), "hello", 2.5, 0.0), gets=("hello", n - 1) if n else ("at", 1.5))
+              sends=(("hello", n), "hello", 3.0, 0.0), gets=("hello", n - 1) if n else ("at", 1.5))
     met_all = [("spread", len(rounds) - 1)]
 
-    S.add("rhs here", [], 0.0, locs["rhs"].wait, gets=("at", 0.5))
     S.add("err here", [], 0.0, locs["err"].wait, gets=("at", 0.5))
     S.add("cof here", [], 0.0, locs["cof"].wait, gets=("at", 1.0))
     S.add("home", [], 0.0, locs["home"].wait, gets=("at", 9.0))
-    S.add("rhs there", [], 0.01, arrivals[0].wait_recv, gets=("at", SWAP_START + SWAP_FIELD))
 
     def err_there():
         arrivals[1].wait_recv()
-        swaps[3].start()
         pl.when(has_prev)(wn_copy.start)
 
     S.add("err there", ["err here"], 0.03, err_there, sends=("next weights", "weights", 4.8, 0.0),
           gets=("at", SWAP_START + 2 * SWAP_FIELD))
     S.add("next weights", [], 0.01, lambda: pl.when(has_next)(wn_copy.wait_recv), gets="next weights")
-    S.add("diagonal", [], 0.6, diagonal, gets=("at", SWAP_START + 1.3 * SWAP_FIELD))
-
-    def piece(n):
-        arrivals[2 + n].wait_recv()
-        if 4 + n < len(swaps):
-            swaps[4 + n].start()
+    S.add("diagonal", [], 0.6, diagonal, gets=("at", 11.5))
 
     for n, k in enumerate(pieces):
-        S.add(("cof", k), ["cof here"], 0.02, functools.partial(piece, n),
+        S.add(("cof", k), ["cof here"], 0.02, arrivals[2 + n].wait_recv,
               gets=("at", SWAP_START + SWAP_FIELD * (2 + 4.0 * (n + 1) / many)))
 
     def whole_rows(it, i, k):
         if it == 0:
-            return ["rhs here", "rhs there"]
+            return []
         return [("image", it - 1, i, k)]
 
-    def edges_out(it, side):
-        k, at = (0, 0) if side == 0 else (final, last)
-        if it == 1:
-            at = 0 if side == 0 else EDGE - 1
-            for i in range(2):
-                eo[it, side, i:i + 1] = image(0, i, k, alone=True)[at:at + 1]
-        else:
-            for i in range(2):
-                eo[it, side, i:i + 1] = states[it][i, at:at + 1]
-        pl.when(ways[side])(edge_copy(eo, ei, h_send, h_recv, it, side).start)
-
-    def adjoint_out(it, side):
-        at = 0 if side == 0 else last
-        here = slice(at, at + 1)
-        go[it, side, 0:1] = c[1, 0, here] * qb[it, here]
-        go[it, side, 1:2] = c[1, 1, here] * qn[it, here]
-        pl.when(ways[side])(edge_copy(go, gi, g_send, g_recv, it, side).start)
+    def adjoint_out(it, side, i):
+        row = edge_row(side)
+        go[it, side, i] = c[1, i, row] * (qn if i else qb)[it, row]
+        pl.when(ways[side])(edge_copy(go, gi, g_send, g_recv, it, side, i).start)
+
+    def edges_in(out, into, ssem, rsem, it, side, i):
+        pl.when(ways[side])(edge_copy(out, into, ssem, rsem, it, side, i).wait_recv)
 
     def store_image(it, i, k):
         y[it, i, rowset(k)] = image(it, i, k)
@@ -447,49 +458,48 @@
 
     for it in range(ITERS):
         for side, k in ((0, 0), (1, final)):
-            if it == 1:
-                needs = [("here", 0, k), ("next", 0, k), ("forth", 0, k), ("adjoint in", 0, side), "diagonal"]
-            else:
-                needs = whole_rows(it, 0, k) + whole_rows(it, 1, k)
-            S.add(("edges out", it, side), needs, 0.12, functools.partial(edges_out, it, side),
-                  sends=(("edges", it, side), ("tile", side), HOP, 0.1))
-            S.add(("edges in", it, side), [], 0.02, lambda it=it, side=side: pl.when(ways[side])(
-                edge_in(eo, ei, h_send, h_recv, it, side).wait_recv), gets=("edges", it, 1 - side))
-            S.add(("adjoint out", it, side), [("here", it, k), ("next", it, k)], 0.06,
-                  functools.partial(adjoint_out, it, side),
-                  sends=(("adjoint", it, side), ("tile", side), HOP, 0.1))
-            S.add(("adjoint in", it, side), [], 0.02, lambda it=it, side=side: pl.when(ways[side])(
-                edge_in(go, gi, g_send, g_recv, it, side).wait_recv), gets=("adjoint", it, 1 - side))
+            for i in range(2):
+                if it > 0:
+                    needs = [("here", it - 1, k), ("adjoint in", it - 1, side, i), "diagonal"]
+                    needs += [("next", it - 1, k)] if i else [("forth", it - 1, k)]
+                    S.add(("edges out", it, side, i), needs, 0.06, functools.partial(edges_out, it, side, i),
+                          sends=(("edges", it, side, i), ("tile", side), TILE_HOPS[side], 0.05))
+                S.add(("edges in", it, side, i), [], 0.02,
+                      functools.partial(edges_in, eo, ei, h_send, h_recv, it, side, i),
+                      gets=("edges", it, side, i) if it else ("at", 7.7))
+                S.add(("adjoint out", it, side, i), [("next" if i else "here", it, k)], 0.03,
+                      functools.partial(adjoint_out, it, side, i),
+                      sends=(("adjoint", it, side, i), ("tile", side), TILE_HOPS[side], 0.05))
+                S.add(("adjoint in", it, side, i), [], 0.02,
+                      functools.partial(edges_in, go, gi, g_send, g_recv, it, side, i),
+                      gets=("adjoint", it, side, i))
         for k in range(blocks):
-            if it == 0:
-                S.add(("back out", 0, k), whole_rows(0, 0, k), 0.02,
-                      lambda k=k: pl.when(has_prev)(back_copy(0, k).start),
-                      sends=(("back", 0, k), "back", HOP, BLOCK))
             S.add(("back", it, k), [], 0.02, lambda it=it, k=k: pl.when(has_next)(
-                back_copy(it, k).wait_recv), gets=("back", it, k))
+                back_copy(it, k).wait_recv),
+                  gets=("back", it, k) if it else ("at", 8.0 + BLOCK * k))
             S.add(("forth", it, k), [], 0.02, lambda it=it, k=k: pl.when(has_prev)(
                 forth_copy(it, k).wait_recv), gets=("forth", it, k))
             around = [m for m in (k - 1, k, k + 1) if 0 <= m < blocks]
             ends = [side for side, m in ((0, 0), (1, final)) if m == k]
             for i in range(2):
-                needs = [("cof", k)] + [("edges in", it, side) for side in ends]
+                needs = [("cof", k)] + [("edges in", it, side, i) for side in ends]
                 for m in around:
                     needs += whole_rows(it, i, m)
                 S.add(("model", it, i, k), needs, 0.05, functools.partial(model, it, i, k),
                       sends=(("forth", it, k), "forth", HOP, BLOCK) if i == 1 else None)
-                needs = ["diagonal", "err here", "err there"] + [("adjoint in", it, side) for side in ends]
+                needs = ["diagonal", "err here", "err there"] + [("adjoint in", it, side, i) for side in ends]
                 needs += [("next" if i else "here", it, m) for m in around]
                 needs += [("here", it, k)] if i else [("forth", it, k)]
                 S.add(("image", it, i, k), needs, 0.06, functools.partial(store_image, it, i, k),
                       sends=(("back", it + 1, k), "back", HOP, BLOCK) if i == 0 and it + 1 < ITERS else None)
-            S.add(("here", it, k), ["err here", "err there", ("model", it, 0, k)], 0.03,
+            S.add(("here", it, k), ["err here", "err there", ("model", it, 0, k)] + whole_rows(it, 1, k), 0.03,
                   functools.partial(misfit_here, it, k))
             S.add(("next", it, k), ["next weights", ("model", it, 1, k), ("back", it, k)], 0.03,
                   functools.partial(misfit_next, it, k))
             S.add(("ret out", it, k), [("image", it, 0, k), ("image", it, 1, k)], 0.02,
                   lambda it=it, k=k: ret_copy(it, k).start(),
                   sends=(("ret", it, k), "ret", HOP, BLOCK))
-            S.add(("ret", it, k), [], 0.01, lambda it=it, k=k: ret_copy(it, k).wait_recv(),
+            S.add(("ret", it, k), ["early in"] if it < 2 else [], 0.01, lambda it=it, k=k: ret_copy(it, k).wait_recv(),
                   gets=("ret", it, k))
 
     def images(it):
@@ -498,19 +508,39 @@
     def moment(n, a, b):
         early[n:n + 1] = lanes(a, b)
 
-    S.add("moment 0", ["rhs here", "rhs there"], 0.15, lambda: moment(0, v, v))
+    S.add("moment 0", [], 0.15, lambda: moment(0, v, v))
     S.add("moment 1", images(0), 0.3, lambda: (moment(1, v, y.at[0]), moment(2, y.at[0], y.at[0])))
     S.add("moment 3", images(1), 0.3,
           lambda: (moment(3, y.at[0], y.at[1]), moment(4, y.at[1], y.at[1])))
 
-    S.add("early out", ["moment 0", "moment 1", "moment 3"] + met_all, 0.4,
+    S.add("early out", ["moment 0", "moment 1", "moment 3", *[("model", 2, 1, k) for k in range(blocks)]] + met_all, 0.4,
           lambda: to_all(early, reds, 0), sends=("early", "all", REDUCE, 0.0))
 
+    def energy_states():
+        total = None
+        first = jnp.where(has_prev, 0.0, 1.0)
+        for k in range(blocks):
+            at = slice(k * EDGE, (k + 1) * EDGE)
+            a, b = states[2][0, at], states[2][1, at]
+            here = (d[0, at] + first * w[0, at]) * (a * a) + d[1, at] * (b * b)
+            total = here if total is None else total + here
+        energy[...] = total
+
+    def energy_misfits(k):
+        at = rowset(k)
+        energy[...] += (qb[2, at] * (states[2][1, at] - u[2, 0, at])
+                        + qn[2, at] * (vn[2, at] - u[2, 1, at]))
+
     def late_out():
-        late[...] = lanes(y.at[1], y.at[2])
+        late[...] = folded(energy[...])
         to_all(late, lasts, 1)
 
-    S.add("late out", images(2) + met_all, 0.5, late_out, sends=("late", "all", REDUCE, 0.0))
+    S.add("energy", images(1), 0.1, energy_states)
+    for k in range(blocks):
+        S.add(("energy", k), ["energy", ("here", 2, k), ("next", 2, k)], 0.04,
+              functools.partial(energy_misfits, k))
+    S.add("late out", [("energy", k) for k in range(blocks)] + met_all, 0.5, late_out,
+          sends=("late", "all", REDUCE, 0.0))
 
     def early_in():
         m = from_all(reds, 0)
@@ -534,7 +564,7 @@
                         pair_scale(rest, p2))
         scalars.update(a0=a0, a1=a1, b1=b1, p1=p1, p2=p2, g2=g2, b2=g2 / g1, base=base)
 
-    S.add("early in", [], 0.6, early_in, gets="early")
+    S.add("early in", ["late out"], 0.6, early_in, gets="early")
 
     def late_in():
         s = scalars
@@ -542,7 +572,7 @@
         d2 = pair_total(pair_add(s["base"], pair_scale(pair_scale(m, s["p2"]), s["p2"])))
         scalars["a2"] = s["g2"] / (d2 - s["b2"] * s["g2"] / s["a1"])
 
-    S.add("late in", ["early in"], 0.4, late_in, gets="late")
+    S.add("late in", ["early in", "sent"], 0.4, late_in, gets="late")
 
     def own(level):
         return lambda at: v[level, at], lambda it, at: y[it, level, at]
@@ -588,6 +618,32 @@
         S.add(("finish away", k), ["late in", ("solve away", k), ("tail away", k)],
               0.04, functools.partial(finish, other, k))
 
+    def sent():
+        for one in swaps:
+            one.wait_send()
+        ob_copy.wait_send()
+        pl.when(has_prev)(wn_copy.wait_send)
+        for it in range(ITERS):
+            for side in range(2):
+                for i in range(2):
+                    pl.when(ways[side])(edge_copy(eo, ei, h_send, h_recv, it, side, i).wait_send)
+                    pl.when(ways[side])(edge_copy(go, gi, g_send, g_recv, it, side, i).wait_send)
+            for k in range(blocks):
+                ret_copy(it, k).wait_send()
+
+            @pl.when(has_prev)
+            def _():
+                for k in range(blocks):
+                    back_copy(it, k).wait_send()
+
+            @pl.when(has_next)
+            def _():
+                for k in range(blocks):
+                    forth_copy(it, k).wait_send()
+        most = reds.at[pl.ds(0, count - 1)]
+        pltpu.make_async_copy(most, most, rd_send.at[0]).wait()
+
+    S.add("sent", [("tail away", k) for k in range(blocks)], 0.5, sent)
     order = S.order()
     if SHOW:
         for name, _, when in order:
@@ -595,30 +651,8 @@
     for name, run, _ in order:
         run()
 
-    for one in swaps:
-        one.wait_send()
-    ob_copy.wait_send()
-    pl.when(has_prev)(wn_copy.wait_send)
-    for it in range(ITERS):
-        for side in range(2):
-            pl.when(ways[side])(edge_copy(eo, ei, h_send, h_recv, it, side).wait_send)
-            pl.when(ways[side])(edge_copy(go, gi, g_send, g_recv, it, side).wait_send)
-        for k in range(blocks):
-            ret_copy(it, k).wait_send()
-
-        @pl.when(has_prev)
-        def _():
-            for k in range(blocks):
-                back_copy(it, k).wait_send()
-
-        @pl.when(has_next)
-        def _():
-            for k in range(blocks):
-                forth_copy(it, k).wait_send()
-
-    for sems, into in ((0, reds), (1, lasts)):
-        most = into.at[pl.ds(0, count - 1)]
-        pltpu.make_async_copy(most, most, rd_send.at[sems]).wait()
+    most = lasts.at[pl.ds(0, count - 1)]
+    pltpu.make_async_copy(most, most, rd_send.at[1]).wait()
 
 
 SHOW = False
@@ -634,7 +668,7 @@
     vmem = pl.BlockSpec(memory_space=pltpu.VMEM)
     blocks = rows // EDGE
     field = (rows, cols)
-    edge = vm((ITERS, 2, 2, cols))
+    edge = vm((ITERS, 2, 2, 1, cols))
     scratch = [
         pltpu.VMEM(obs_block.shape, jnp.int32),
         pltpu.VMEM(obs_pos.shape, jnp.int32),
@@ -656,14 +690,15 @@
         vm(field),
         vm((2,) + field),
         vm((2,) + field),
+        vm((EDGE, cols)),
         vm((MOMENTS, width)),
         vm((1, width)),
         vm((wins * tiles, MOMENTS, width)),
         vm((wins * tiles, 1, width)),
         dma((3 + blocks,)), dma((3 + blocks,)), dma((7,)),
-        dma((ITERS, 2)), dma((ITERS, 2)),
+        dma((ITERS, 2, 2)), dma((ITERS, 2, 2)),
         dma((2, ITERS, blocks)), dma((2, ITERS, blocks)),
-        dma((ITERS, 2)), dma((ITERS, 2)),
+        dma((ITERS, 2, 2)), dma((ITERS, 2, 2)),
         dma((ITERS, blocks)), dma((ITERS, blocks)),
         dma((2,)), dma((2,)),
         dma, dma,

time: 46.2 us -> 41.8 us (0.905)
  Pallas kernels: 44 us -> 39.6 us
    pallas_call x1, Pallas kernels: 44 us -> 39.6 us  [on_device(): pl.pallas_call(functools.partial(kernel, wins, tiles), out_shape=(out, ou...]
where the time goes in v2:
time: 41.8 us; the launch traced here: 41.6 us
  Pallas kernels  39.6 us (95%)
  local copies, waits for them, and re-layouts  1.41 us (3%)
  between operations  0.64 us (2%)
    pallas_call x1, Pallas kernels, on_device(): pl.pallas_call(functools.partial(kernel, wins, tiles), out_shape=(out, ou...  39.6 us
    unnamed x2, local copies, waits for them, and re-layouts  1.41 us

profile of v2, /device:TPU:0, one launch (start us, length us, event | category | flops | bytes accessed | tf_op | source)
XLA Modules:
  0.0 41.6 jit_solution(2932448606383027196)
XLA Ops:
  0.6 39.6 %shard_map.77 = (f32[1,2,32,1024]{3,2,1,0:T(8,128)S(1)}, f32[1,2,32,1024]{3,2,1,0:T(8,128)S(1)}) custom-call(f32[1,2,32,1024]{3,2,1,0:T(8,128)} %rhs.1, f32[1,2,32,1024]{3,2,1,0:T(8,128)} %err.1, f32[4,1,2,32,1024]{4,3,2,1,0:T(8,128)} %cof.1, s32[1,32]{1,0:T(1,128)} %oblk_in.1, s32[1,32,128]{2,1,0:T(8,128)} %opos_in.1, f32[1,32,128]{2,1,0:T(8,128)} %owgt_in.1), custom_call_target="tpu_custom_call" | custom-call | tf_op jit(solution)/shard_map/pallas_call | solution.py:708
  40.2 0.7 %copy.10 = f32[1,2,32,1024]{3,2,1,0:T(8,128)} copy(f32[1,2,32,1024]{3,2,1,0:T(8,128)S(1)} %get-tuple-element.2) | data formatting | bytes 524288
  40.9 0.7 %copy.11 = f32[1,2,32,1024]{3,2,1,0:T(8,128)} copy(f32[1,2,32,1024]{3,2,1,0:T(8,128)S(1)} %get-tuple-element.3) | data formatting | bytes 524288

commit v3 on v2

--- a/solution.py
+++ b/solution.py
@@ -123,7 +123,7 @@
 def kernel(wins, tiles, rhs, err, cof, oblk_in, opos_in, owgt_in, x_out, r_out,
            obk, ops, owt, v, y, w, wn, c, d, ob, u, ui, vn, qb, qn, eo, ei, go, gi, rt, home,
            step, grad, energy, early, late, reds, lasts,
-           x_sem, xs_sem, l_sem, h_send, h_recv, b_send, b_recv, g_send, g_recv,
+           x_sem, xs_sem, l_sem, f_recv, h_send, h_recv, b_send, b_recv, c_recv, g_send, g_recv,
            rt_send, rt_recv, rd_send, rd_recv, wn_send, wn_recv, hello):
     me_w = lax.axis_index("win")
     me_t = lax.axis_index("tile")
@@ -167,6 +167,9 @@
             src_ref=src, dst_ref=dst, send_sem=ssem, recv_sem=rsem,
             device_id=(win, tile), device_id_type=pl.DeviceIdType.MESH)
 
+    def all_of(ref, sem):
+        return pltpu.make_async_copy(ref, ref, sem)
+
     barrier = pltpu.get_barrier_semaphore()
 
     def signal(sem, win, tile):
@@ -195,27 +198,27 @@
 
     swaps = [
         remote(rhs.at[0, other], v.at[lev], xs_sem.at[0], x_sem.at[0], mate, me_t),
-        remote(err.at[0, other], w.at[lev], xs_sem.at[1], x_sem.at[1], mate, me_t),
+        remote(err.at[0, other], w.at[lev], xs_sem.at[0], x_sem.at[1], mate, me_t),
     ] + [
         remote(cof.at[:, 0, other, rowset(k)], c.at[:, lev, rowset(k)],
-               xs_sem.at[3 + n], x_sem.at[3 + n], mate, me_t)
+               xs_sem.at[0], x_sem.at[3 + n], mate, me_t)
         for n, k in enumerate(pieces)
     ]
     arrivals = [
         remote(rhs.at[0, other], v.at[other], xs_sem.at[0], x_sem.at[0], mate, me_t),
-        remote(err.at[0, other], w.at[other], xs_sem.at[1], x_sem.at[1], mate, me_t),
+        remote(err.at[0, other], w.at[other], xs_sem.at[0], x_sem.at[1], mate, me_t),
     ] + [
         remote(cof.at[:, 0, other, rowset(k)], c.at[:, other, rowset(k)],
-               xs_sem.at[3 + n], x_sem.at[3 + n], mate, me_t)
+               xs_sem.at[0], x_sem.at[3 + n], mate, me_t)
         for n, k in enumerate(pieces)
     ]
     locs = {
-        "block": pltpu.make_async_copy(oblk_in, obk, l_sem.at[4]),
-        "pos": pltpu.make_async_copy(opos_in, ops, l_sem.at[5]),
-        "weight": pltpu.make_async_copy(owgt_in, owt, l_sem.at[6]),
-        "rhs": pltpu.make_async_copy(rhs.at[0, lev], v.at[lev], l_sem.at[0]),
-        "err": pltpu.make_async_copy(err.at[0, lev], w.at[lev], l_sem.at[1]),
-        "home": pltpu.make_async_copy(rhs.at[0, other], home, l_sem.at[2]),
+        "block": pltpu.make_async_copy(oblk_in, obk, l_sem.at[0]),
+        "pos": pltpu.make_async_copy(opos_in, ops, l_sem.at[1]),
+        "weight": pltpu.make_async_copy(owgt_in, owt, l_sem.at[4]),
+        "rhs": pltpu.make_async_copy(rhs.at[0, lev], v.at[lev], l_sem.at[2]),
+        "err": pltpu.make_async_copy(err.at[0, lev], w.at[lev], l_sem.at[3]),
+        "home": pltpu.make_async_copy(rhs.at[0, other], home, l_sem.at[3]),
         "cof": pltpu.make_async_copy(cof.at[:, 0, lev], c.at[:, lev], l_sem.at[3]),
     }
     for one in locs.values():
@@ -258,20 +261,27 @@
                 + jnp.where(row8 == EDGE - 1, bottom, pltpu.roll(a, EDGE - 1, 0)))
 
     def edge_copy(out, into, ssem, rsem, it, side, i):
-        return remote(out.at[it, side, i], into.at[it, side, i], ssem.at[it, side, i],
-                      rsem.at[it, side, i], me_w, beside[side])
+        return remote(out.at[it, side, i], into.at[it, side, i], ssem.at[side],
+                      rsem(it, side, i), me_w, beside[side])
+
+    def edge_sem(it, side, i):
+        return f_recv.at[side] if it == 0 else h_recv.at[it - 1, side, i]
+
+    def adjoint_sem(it, side, i):
+        return g_recv.at[it, side, i]
+
 
     def back_copy(it, k):
         return remote(states[it].at[0, rowset(k)], vn.at[it, rowset(k)],
-                      b_send.at[0, it, k], b_recv.at[0, it, k], me_w - 2, me_t)
+                      b_send.at[0], b_recv.at[it - 1, k] if it else f_recv.at[2], me_w - 2, me_t)
 
     def forth_copy(it, k):
         return remote(u.at[it, 1, rowset(k)], ui.at[it, rowset(k)],
-                      b_send.at[1, it, k], b_recv.at[1, it, k], me_w + 2, me_t)
+                      b_send.at[1], c_recv.at[it, k], me_w + 2, me_t)
 
     def ret_copy(it, k):
         return remote(y.at[it, other, rowset(k)], rt.at[it, rowset(k)],
-                      rt_send.at[it, k], rt_recv.at[it, k], mate, me_t)
+                      rt_send, rt_recv.at[k if it == ITERS - 1 else blocks], mate, me_t)
 
     wn_copy = remote(w.at[0], wn, wn_send, wn_recv, me_w - 2, me_t)
 
@@ -374,7 +384,7 @@
             whole = image(it - 1, i, 0 if side == 0 else final, alone=True)
             low, high = whole[0:1], whole[EDGE - 1:EDGE]
             eo[it, side, i] = jnp.where(even, low, high) if side == 0 else jnp.where(even, high, low)
-        pl.when(ways[side])(edge_copy(eo, ei, h_send, h_recv, it, side, i).start)
+        pl.when(ways[side])(edge_copy(eo, ei, h_send, edge_sem, it, side, i).start)
 
     for one in ("block", "pos", "weight"):
         locs[one].wait()
@@ -402,8 +412,8 @@
             edges_out(0, side, i)
     lax.fori_loop(most, nblk, per_block, 0)
     ob[lev, nblk:nblk + 1, 0:nblk] = obk[...].astype(f32)
-    ob_copy = remote(ob.at[lev], ob.at[lev], xs_sem.at[2], x_sem.at[2], mate, me_t)
-    ob_back = remote(ob.at[lev], ob.at[other], xs_sem.at[2], x_sem.at[2], mate, me_t)
+    ob_copy = remote(ob.at[lev], ob.at[lev], xs_sem.at[1], x_sem.at[2], mate, me_t)
+    ob_back = remote(ob.at[lev], ob.at[other], xs_sem.at[1], x_sem.at[2], mate, me_t)
     ob_copy.start()
     for one in swaps[4:]:
         one.start()
@@ -421,21 +431,19 @@
               sends=(("hello", n), "hello", 3.0, 0.0), gets=("hello", n - 1) if n else ("at", 1.5))
     met_all = [("spread", len(rounds) - 1)]
 
-    S.add("err here", [], 0.0, locs["err"].wait, gets=("at", 0.5))
-    S.add("cof here", [], 0.0, locs["cof"].wait, gets=("at", 1.0))
-    S.add("home", [], 0.0, locs["home"].wait, gets=("at", 9.0))
+    S.add("here", [], 0.01, all_of(y, l_sem.at[3]).wait, gets=("at", 1.0))
 
     def err_there():
         arrivals[1].wait_recv()
         pl.when(has_prev)(wn_copy.start)
 
-    S.add("err there", ["err here"], 0.03, err_there, sends=("next weights", "weights", 4.8, 0.0),
+    S.add("err there", ["here"], 0.03, err_there, sends=("next weights", "weights", 4.8, 0.0),
           gets=("at", SWAP_START + 2 * SWAP_FIELD))
     S.add("next weights", [], 0.01, lambda: pl.when(has_next)(wn_copy.wait_recv), gets="next weights")
     S.add("diagonal", [], 0.6, diagonal, gets=("at", 11.5))
 
     for n, k in enumerate(pieces):
-        S.add(("cof", k), ["cof here"], 0.02, arrivals[2 + n].wait_recv,
+        S.add(("cof", k), ["here"], 0.02, arrivals[2 + n].wait_recv,
               gets=("at", SWAP_START + SWAP_FIELD * (2 + 4.0 * (n + 1) / many)))
 
     def whole_rows(it, i, k):
@@ -446,7 +454,7 @@
     def adjoint_out(it, side, i):
         row = edge_row(side)
         go[it, side, i] = c[1, i, row] * (qn if i else qb)[it, row]
-        pl.when(ways[side])(edge_copy(go, gi, g_send, g_recv, it, side, i).start)
+        pl.when(ways[side])(edge_copy(go, gi, g_send, adjoint_sem, it, side, i).start)
 
     def edges_in(out, into, ssem, rsem, it, side, i):
         pl.when(ways[side])(edge_copy(out, into, ssem, rsem, it, side, i).wait_recv)
@@ -464,43 +472,52 @@
                     needs += [("next", it - 1, k)] if i else [("forth", it - 1, k)]
                     S.add(("edges out", it, side, i), needs, 0.06, functools.partial(edges_out, it, side, i),
                           sends=(("edges", it, side, i), ("tile", side), TILE_HOPS[side], 0.05))
-                S.add(("edges in", it, side, i), [], 0.02,
-                      functools.partial(edges_in, eo, ei, h_send, h_recv, it, side, i),
-                      gets=("edges", it, side, i) if it else ("at", 7.7))
+                if it > 0:
+                    S.add(("edges in", it, side, i), [], 0.02,
+                          functools.partial(edges_in, eo, ei, h_send, edge_sem, it, side, i),
+                          gets=("edges", it, side, i))
+                elif i == 0:
+                    S.add(("edges in", 0, side), [], 0.02, functools.partial(
+                        pl.when(ways[side]), all_of(ei.at[0, side], f_recv.at[side]).wait), gets=("at", 7.7))
                 S.add(("adjoint out", it, side, i), [("next" if i else "here", it, k)], 0.03,
                       functools.partial(adjoint_out, it, side, i),
                       sends=(("adjoint", it, side, i), ("tile", side), TILE_HOPS[side], 0.05))
                 S.add(("adjoint in", it, side, i), [], 0.02,
-                      functools.partial(edges_in, go, gi, g_send, g_recv, it, side, i),
+                      functools.partial(edges_in, go, gi, g_send, adjoint_sem, it, side, i),
                       gets=("adjoint", it, side, i))
         for k in range(blocks):
-            S.add(("back", it, k), [], 0.02, lambda it=it, k=k: pl.when(has_next)(
-                back_copy(it, k).wait_recv),
-                  gets=("back", it, k) if it else ("at", 8.0 + BLOCK * k))
+            if it > 0:
+                S.add(("back", it, k), [], 0.02, lambda it=it, k=k: pl.when(has_next)(
+                    back_copy(it, k).wait_recv), gets=("back", it, k))
+            elif k == 0:
+                S.add(("back", 0), [], 0.02, functools.partial(
+                    pl.when(has_next), all_of(vn.at[0], f_recv.at[2]).wait), gets=("at", 10.2))
             S.add(("forth", it, k), [], 0.02, lambda it=it, k=k: pl.when(has_prev)(
                 forth_copy(it, k).wait_recv), gets=("forth", it, k))
             around = [m for m in (k - 1, k, k + 1) if 0 <= m < blocks]
             ends = [side for side, m in ((0, 0), (1, final)) if m == k]
             for i in range(2):
-                needs = [("cof", k)] + [("edges in", it, side, i) for side in ends]
+                needs = [("cof", k)] + [("edges in", it, side) + ((i,) if it else ()) for side in ends]
                 for m in around:
                     needs += whole_rows(it, i, m)
                 S.add(("model", it, i, k), needs, 0.05, functools.partial(model, it, i, k),
                       sends=(("forth", it, k), "forth", HOP, BLOCK) if i == 1 else None)
-                needs = ["diagonal", "err here", "err there"] + [("adjoint in", it, side, i) for side in ends]
+                needs = ["diagonal", "here", "err there"] + [("adjoint in", it, side, i) for side in ends]
                 needs += [("next" if i else "here", it, m) for m in around]
                 needs += [("here", it, k)] if i else [("forth", it, k)]
                 S.add(("image", it, i, k), needs, 0.06, functools.partial(store_image, it, i, k),
                       sends=(("back", it + 1, k), "back", HOP, BLOCK) if i == 0 and it + 1 < ITERS else None)
-            S.add(("here", it, k), ["err here", "err there", ("model", it, 0, k)] + whole_rows(it, 1, k), 0.03,
+            S.add(("here", it, k), ["here", "err there", ("model", it, 0, k)] + whole_rows(it, 1, k), 0.03,
                   functools.partial(misfit_here, it, k))
-            S.add(("next", it, k), ["next weights", ("model", it, 1, k), ("back", it, k)], 0.03,
+            S.add(("next", it, k), ["next weights", ("model", it, 1, k), ("back", it) + ((k,) if it else ())], 0.03,
                   functools.partial(misfit_next, it, k))
             S.add(("ret out", it, k), [("image", it, 0, k), ("image", it, 1, k)], 0.02,
                   lambda it=it, k=k: ret_copy(it, k).start(),
                   sends=(("ret", it, k), "ret", HOP, BLOCK))
-            S.add(("ret", it, k), ["early in"] if it < 2 else [], 0.01, lambda it=it, k=k: ret_copy(it, k).wait_recv(),
-                  gets=("ret", it, k))
+            if it == ITERS - 1:
+                S.add(("ret", it, k), [], 0.01, ret_copy(it, k).wait_recv, gets=("ret", it, k))
+
+    S.add("ret", ["early in"], 0.01, all_of(rt.at[pl.ds(0, ITERS - 1)], rt_recv.at[blocks]).wait)
 
     def images(it):
         return [("image", it, i, k) for i in range(2) for k in range(blocks)]
@@ -607,11 +624,11 @@
     for k in range(blocks):
         S.add(("solve own", k), ["early in"] + [("image", it, i, k) for it in range(2) for i in range(2)],
               0.06, functools.partial(solve, lev, own(lev), k))
-        S.add(("solve away", k), ["early in", "home"] + [("ret", it, k) for it in range(2)],
+        S.add(("solve away", k), ["early in", "here", "ret"],
               0.06, functools.partial(solve, other, away(), k))
         S.add(("tail own", k), ["early in"] + [("image", it, i, k) for it in range(3) for i in range(2)],
               0.06, functools.partial(tail, lev, own(lev), k))
-        S.add(("tail away", k), ["early in"] + [("ret", it, k) for it in range(3)],
+        S.add(("tail away", k), ["early in", "ret", ("ret", ITERS - 1, k)],
               0.06, functools.partial(tail, other, away(), k))
         S.add(("finish own", k), ["late in", ("solve own", k), ("tail own", k)],
               0.04, functools.partial(finish, lev, k))
@@ -619,29 +636,16 @@
               0.04, functools.partial(finish, other, k))
 
     def sent():
-        for one in swaps:
-            one.wait_send()
+        all_of(y, xs_sem.at[0]).wait()
         ob_copy.wait_send()
         pl.when(has_prev)(wn_copy.wait_send)
-        for it in range(ITERS):
-            for side in range(2):
-                for i in range(2):
-                    pl.when(ways[side])(edge_copy(eo, ei, h_send, h_recv, it, side, i).wait_send)
-                    pl.when(ways[side])(edge_copy(go, gi, g_send, g_recv, it, side, i).wait_send)
-            for k in range(blocks):
-                ret_copy(it, k).wait_send()
-
-            @pl.when(has_prev)
-            def _():
-                for k in range(blocks):
-                    back_copy(it, k).wait_send()
-
-            @pl.when(has_next)
-            def _():
-                for k in range(blocks):
-                    forth_copy(it, k).wait_send()
-        most = reds.at[pl.ds(0, count - 1)]
-        pltpu.make_async_copy(most, most, rd_send.at[0]).wait()
+        for side in range(2):
+            pl.when(ways[side])(all_of(eo.at[:, side], h_send.at[side]).wait)
+            pl.when(ways[side])(all_of(go.at[:, side], g_send.at[side]).wait)
+        all_of(rt, rt_send).wait()
+        pl.when(has_prev)(all_of(vn, b_send.at[0]).wait)
+        pl.when(has_next)(all_of(ui, b_send.at[1]).wait)
+        all_of(reds.at[pl.ds(0, count - 1)], rd_send.at[0]).wait()
 
     S.add("sent", [("tail away", k) for k in range(blocks)], 0.5, sent)
     order = S.order()
@@ -695,11 +699,11 @@
         vm((1, width)),
         vm((wins * tiles, MOMENTS, width)),
         vm((wins * tiles, 1, width)),
-        dma((3 + blocks,)), dma((3 + blocks,)), dma((7,)),
-        dma((ITERS, 2, 2)), dma((ITERS, 2, 2)),
-        dma((2, ITERS, blocks)), dma((2, ITERS, blocks)),
-        dma((ITERS, 2, 2)), dma((ITERS, 2, 2)),
-        dma((ITERS, blocks)), dma((ITERS, blocks)),
+        dma((3 + blocks,)), dma((2,)), dma((5,)),
+        dma((3,)), dma((2,)), dma((ITERS - 1, 2, 2)),
+        dma((2,)), dma((ITERS - 1, blocks)), dma((ITERS, blocks)),
+        dma((2,)), dma((ITERS, 2, 2)),
+        dma, dma((1 + blocks,)),
         dma((2,)), dma((2,)),
         dma, dma,
         pltpu.SemaphoreType.REGULAR((1 + len(doubling(tiles)) + len(doubling(wins // 2)),)),

time: 41.8 us -> 41 us (0.981)
  Pallas kernels: 39.6 us -> 38.8 us
    pallas_call x1, Pallas kernels: 39.6 us -> 38.8 us  [on_device(): pl.pallas_call(functools.partial(kernel, wins, tiles), out_shape=(out, ou...]
where the time goes in v3:
time: 41 us; the launch traced here: 40.9 us
  Pallas kernels  38.8 us (95%)
  local copies, waits for them, and re-layouts  1.41 us (3%)
  between operations  0.64 us (2%)
    pallas_call x1, Pallas kernels, on_device(): pl.pallas_call(functools.partial(kernel, wins, tiles), out_shape=(out, ou...  38.8 us
    unnamed x2, local copies, waits for them, and re-layouts  1.41 us

profile of v3, /device:TPU:0, one launch (start us, length us, event | category | flops | bytes accessed | tf_op | source)
XLA Modules:
  0.0 40.9 jit_solution(12479845613716563295)
XLA Ops:
  0.6 38.8 %shard_map.77 = (f32[1,2,32,1024]{3,2,1,0:T(8,128)S(1)}, f32[1,2,32,1024]{3,2,1,0:T(8,128)S(1)}) custom-call(f32[1,2,32,1024]{3,2,1,0:T(8,128)} %rhs.1, f32[1,2,32,1024]{3,2,1,0:T(8,128)} %err.1, f32[4,1,2,32,1024]{4,3,2,1,0:T(8,128)} %cof.1, s32[1,32]{1,0:T(1,128)} %oblk_in.1, s32[1,32,128]{2,1,0:T(8,128)} %opos_in.1, f32[1,32,128]{2,1,0:T(8,128)} %owgt_in.1), custom_call_target="tpu_custom_call" | custom-call | tf_op jit(solution)/shard_map/pallas_call | solution.py:712
  39.5 0.7 %copy.10 = f32[1,2,32,1024]{3,2,1,0:T(8,128)} copy(f32[1,2,32,1024]{3,2,1,0:T(8,128)S(1)} %get-tuple-element.2) | data formatting | bytes 524288
  40.2 0.7 %copy.11 = f32[1,2,32,1024]{3,2,1,0:T(8,128)} copy(f32[1,2,32,1024]{3,2,1,0:T(8,128)S(1)} %get-tuple-element.3) | data formatting | bytes 524288

commit v4 on v3

--- a/solution.py
+++ b/solution.py
@@ -11,7 +11,7 @@
 EDGE = 8
 MOMENTS = 2 * ITERS - 1
 
-HOP, TILE_HOPS, BLOCK, SWAP_START, SWAP_FIELD, REDUCE, BEGIN = 2.2, (2.8, 1.5), 0.7, 2.2, 2.83, 5.2, 7.5
+HOP, TILE_HOPS, BLOCK, SWAP_START, SWAP_FIELD, REDUCE, BEGIN = 2.40, (3.30, 1.50), 0.70, 2.20, 2.83, 5.31, 7.50
 
 
 def doubling(length):
@@ -20,6 +20,10 @@
         steps.append(known)
         known *= 2
     return steps
+
+
+HINTS = {('back', 2): -1.4, 'early out': 1.3, ('model', 1): -0.87}
+STEP = 1.00
 
 
 class Steps:
@@ -47,6 +51,9 @@
 
         for name in self.todo:
             path(name)
+        for name in self.todo:
+            kind = name if isinstance(name, str) else name[:2]
+            rank[name] += HINTS.get(kind, 0.0)
         now, done, arrive, free, result = BEGIN, set(), {}, {}, []
         for _, (_, _, _, _, gets) in self.todo.items():
             if isinstance(gets, tuple) and gets[0] == "at":
@@ -69,7 +76,7 @@
             if pick is None:
                 now, pick = soon
             _, cost, run, sends, _ = left.pop(pick)
-            now += cost
+            now += STEP * cost
             done.add(pick)
             if sends:
                 message, link, latency, busy = sends
@@ -121,7 +128,7 @@
 
 
 def kernel(wins, tiles, rhs, err, cof, oblk_in, opos_in, owgt_in, x_out, r_out,
-           obk, ops, owt, v, y, w, wn, c, d, ob, u, ui, vn, qb, qn, eo, ei, go, gi, rt, home,
+           obk, ops, owt, v, y, w, wn, c, d, ob, u, ui, vn, qb, qn, eo, ei, go, gi, rt, home, far, ahead,
            step, grad, energy, early, late, reds, lasts,
            x_sem, xs_sem, l_sem, f_recv, h_send, h_recv, b_send, b_recv, c_recv, g_send, g_recv,
            rt_send, rt_recv, rd_send, rd_recv, wn_send, wn_recv, hello):
@@ -220,6 +227,7 @@
         "err": pltpu.make_async_copy(err.at[0, lev], w.at[lev], l_sem.at[3]),
         "home": pltpu.make_async_copy(rhs.at[0, other], home, l_sem.at[3]),
         "cof": pltpu.make_async_copy(cof.at[:, 0, lev], c.at[:, lev], l_sem.at[3]),
+        "far": pltpu.make_async_copy(cof.at[:, 0, other, rowset(pieces[-1])], far, l_sem.at[5]),
     }
     for one in locs.values():
         one.start()
@@ -277,11 +285,17 @@
 
     def forth_copy(it, k):
         return remote(u.at[it, 1, rowset(k)], ui.at[it, rowset(k)],
-                      b_send.at[1], c_recv.at[it, k], me_w + 2, me_t)
+                      b_send.at[2 if it else 1], c_recv.at[it, k], me_w + 2, me_t)
 
     def ret_copy(it, k):
         return remote(y.at[it, other, rowset(k)], rt.at[it, rowset(k)],
                       rt_send, rt_recv.at[k if it == ITERS - 1 else blocks], mate, me_t)
+
+    sends_ahead = jnp.logical_and(lev == 1, has_next)
+
+    def ahead_copy(n):
+        return remote(ahead.at[n], ui.at[0, rowset(pieces[-1])], b_send.at[3],
+                      c_recv.at[0, pieces[-1]], me_w + 2 - n, me_t)
 
     wn_copy = remote(w.at[0], wn, wn_send, wn_recv, me_w - 2, me_t)
 
@@ -295,7 +309,7 @@
                   for side in range(2)]
         u[it, i, at] = (c[0, i, at] * a + c[1, i, at] * sides(a, beyond)
                         + c[2, i, at] * east(a) + c[3, i, at] * west(a))
-        if i == 1:
+        if i == 1 and (it, k) != (0, pieces[-1]):
             pl.when(has_next)(forth_copy(it, k).start)
 
     def misfit_here(it, k):
@@ -410,6 +424,19 @@
     for side in range(2):
         for i in range(2):
             edges_out(0, side, i)
+    all_of(y, l_sem.at[3]).wait()
+    locs["far"].wait()
+
+    @pl.when(sends_ahead)
+    def _():
+        at = rowset(pieces[-1])
+        rims = [row_beyond(pieces[-1], side) for side in range(2)]
+        for n, (a, beyond, k) in enumerate((
+                (v[lev, at], [v[lev, row] for row in rims], [c[m, lev, at] for m in range(4)]),
+                (home[at], [home[row] for row in rims], [far[m] for m in range(4)]))):
+            ahead[n] = k[0] * a + k[1] * sides(a, beyond) + k[2] * east(a) + k[3] * west(a)
+            ahead_copy(n).start()
+
     lax.fori_loop(most, nblk, per_block, 0)
     ob[lev, nblk:nblk + 1, 0:nblk] = obk[...].astype(f32)
     ob_copy = remote(ob.at[lev], ob.at[lev], xs_sem.at[1], x_sem.at[2], mate, me_t)
@@ -431,7 +458,7 @@
               sends=(("hello", n), "hello", 3.0, 0.0), gets=("hello", n - 1) if n else ("at", 1.5))
     met_all = [("spread", len(rounds) - 1)]
 
-    S.add("here", [], 0.01, all_of(y, l_sem.at[3]).wait, gets=("at", 1.0))
+    S.add("here", [], 0.0, lambda: None)
 
     def err_there():
         arrivals[1].wait_recv()
@@ -440,7 +467,7 @@
     S.add("err there", ["here"], 0.03, err_there, sends=("next weights", "weights", 4.8, 0.0),
           gets=("at", SWAP_START + 2 * SWAP_FIELD))
     S.add("next weights", [], 0.01, lambda: pl.when(has_next)(wn_copy.wait_recv), gets="next weights")
-    S.add("diagonal", [], 0.6, diagonal, gets=("at", 11.5))
+    S.add("diagonal", [], 0.6, diagonal, gets=("at", 15.2))
 
     for n, k in enumerate(pieces):
         S.add(("cof", k), ["here"], 0.02, arrivals[2 + n].wait_recv,
@@ -493,7 +520,8 @@
                 S.add(("back", 0), [], 0.02, functools.partial(
                     pl.when(has_next), all_of(vn.at[0], f_recv.at[2]).wait), gets=("at", 10.2))
             S.add(("forth", it, k), [], 0.02, lambda it=it, k=k: pl.when(has_prev)(
-                forth_copy(it, k).wait_recv), gets=("forth", it, k))
+                forth_copy(it, k).wait_recv),
+                  gets=("at", 10.5) if (it, k) == (0, pieces[-1]) else ("forth", it, k))
             around = [m for m in (k - 1, k, k + 1) if 0 <= m < blocks]
             ends = [side for side, m in ((0, 0), (1, final)) if m == k]
             for i in range(2):
@@ -501,7 +529,8 @@
                 for m in around:
                     needs += whole_rows(it, i, m)
                 S.add(("model", it, i, k), needs, 0.05, functools.partial(model, it, i, k),
-                      sends=(("forth", it, k), "forth", HOP, BLOCK) if i == 1 else None)
+                      sends=(("forth", it, k), "forth", HOP, BLOCK)
+                      if i == 1 and (it, k) != (0, pieces[-1]) else None)
                 needs = ["diagonal", "here", "err there"] + [("adjoint in", it, side, i) for side in ends]
                 needs += [("next" if i else "here", it, m) for m in around]
                 needs += [("here", it, k)] if i else [("forth", it, k)]
@@ -644,22 +673,18 @@
             pl.when(ways[side])(all_of(go.at[:, side], g_send.at[side]).wait)
         all_of(rt, rt_send).wait()
         pl.when(has_prev)(all_of(vn, b_send.at[0]).wait)
-        pl.when(has_next)(all_of(ui, b_send.at[1]).wait)
+        pl.when(has_next)(all_of(ui.at[0, pl.ds(0, rows - EDGE)], b_send.at[1]).wait)
+        pl.when(has_next)(all_of(ui.at[pl.ds(1, ITERS - 1)], b_send.at[2]).wait)
+        pl.when(sends_ahead)(all_of(ahead, b_send.at[3]).wait)
         all_of(reds.at[pl.ds(0, count - 1)], rd_send.at[0]).wait()
 
     S.add("sent", [("tail away", k) for k in range(blocks)], 0.5, sent)
     order = S.order()
-    if SHOW:
-        for name, _, when in order:
-            print(f"{when:6.2f}", name)
     for name, run, _ in order:
         run()
 
     most = lasts.at[pl.ds(0, count - 1)]
     pltpu.make_async_copy(most, most, rd_send.at[1]).wait()
-
-
-SHOW = False
 
 
 def on_device(wins, tiles, right_side, error_weight, coeffs, obs_block, obs_pos, obs_weight):
@@ -692,6 +717,8 @@
         edge, edge, edge, edge,
         vm((ITERS,) + field),
         vm(field),
+        vm((4, EDGE, cols)),
+        vm((2, EDGE, cols)),
         vm((2,) + field),
         vm((2,) + field),
         vm((EDGE, cols)),
@@ -699,9 +726,9 @@
         vm((1, width)),
         vm((wins * tiles, MOMENTS, width)),
         vm((wins * tiles, 1, width)),
-        dma((3 + blocks,)), dma((2,)), dma((5,)),
+        dma((3 + blocks,)), dma((2,)), dma((6,)),
         dma((3,)), dma((2,)), dma((ITERS - 1, 2, 2)),
-        dma((2,)), dma((ITERS - 1, blocks)), dma((ITERS, blocks)),
+        dma((4,)), dma((ITERS - 1, blocks)), dma((ITERS, blocks)),
         dma((2,)), dma((ITERS, 2, 2)),
         dma, dma((1 + blocks,)),
         dma((2,)), dma((2,)),

time: 41 us -> 40 us (0.976)
  Pallas kernels: 38.8 us -> 37.9 us
    pallas_call x1, Pallas kernels: 38.8 us -> 37.9 us  [on_device(): pl.pallas_call(functools.partial(kernel, wins, tiles), out_shape=(out, ou...]
where the time goes in v4:
time: 40 us; the launch traced here: 39.9 us
  Pallas kernels  37.9 us (95%)
  local copies, waits for them, and re-layouts  1.41 us (4%)
  between operations  0.64 us (2%)
    pallas_call x1, Pallas kernels, on_device(): pl.pallas_call(functools.partial(kernel, wins, tiles), out_shape=(out, ou...  37.9 us
    unnamed x2, local copies, waits for them, and re-layouts  1.41 us

profile of v4, /device:TPU:0, one launch (start us, length us, event | category | flops | bytes accessed | tf_op | source)
XLA Modules:
  0.0 39.9 jit_solution(8695015983613071669)
XLA Ops:
  0.6 37.9 %shard_map.77 = (f32[1,2,32,1024]{3,2,1,0:T(8,128)S(1)}, f32[1,2,32,1024]{3,2,1,0:T(8,128)S(1)}) custom-call(f32[1,2,32,1024]{3,2,1,0:T(8,128)} %rhs.1, f32[1,2,32,1024]{3,2,1,0:T(8,128)} %err.1, f32[4,1,2,32,1024]{4,3,2,1,0:T(8,128)} %cof.1, s32[1,32]{1,0:T(1,128)} %oblk_in.1, s32[1,32,128]{2,1,0:T(8,128)} %opos_in.1, f32[1,32,128]{2,1,0:T(8,128)} %owgt_in.1), custom_call_target="tpu_custom_call" | custom-call | tf_op jit(solution)/shard_map/pallas_call | solution.py:739
  38.5 0.7 %copy.10 = f32[1,2,32,1024]{3,2,1,0:T(8,128)} copy(f32[1,2,32,1024]{3,2,1,0:T(8,128)S(1)} %get-tuple-element.2) | data formatting | bytes 524288
  39.2 0.7 %copy.11 = f32[1,2,32,1024]{3,2,1,0:T(8,128)} copy(f32[1,2,32,1024]{3,2,1,0:T(8,128)S(1)} %get-tuple-element.3) | data formatting | bytes 524288

commit v5 on v4

--- a/solution.py
+++ b/solution.py
@@ -414,7 +414,7 @@
         ob[lev, pl.ds(b, 1), :] = total[0:1]
         return carry
 
-    most = nblk - nblk // 4
+    most = nblk // 2
     lax.fori_loop(0, most, per_block, 0)
     locs["rhs"].wait()
     arrivals[0].wait_recv()

time: 40 us -> 40 us (level)
  no operation moved by 1% of the time
where the time goes in v5:
time: 40 us; the launch traced here: 39.9 us
  Pallas kernels  37.9 us (95%)
  local copies, waits for them, and re-layouts  1.41 us (4%)
  between operations  0.64 us (2%)
    pallas_call x1, Pallas kernels, on_device(): pl.pallas_call(functools.partial(kernel, wins, tiles), out_shape=(out, ou...  37.9 us
    unnamed x2, local copies, waits for them, and re-layouts  1.41 us

profile of v5, /device:TPU:0, one launch (start us, length us, event | category | flops | bytes accessed | tf_op | source)
XLA Modules:
  0.0 39.9 jit_solution(18342650879625686526)
XLA Ops:
  0.6 37.9 %shard_map.77 = (f32[1,2,32,1024]{3,2,1,0:T(8,128)S(1)}, f32[1,2,32,1024]{3,2,1,0:T(8,128)S(1)}) custom-call(f32[1,2,32,1024]{3,2,1,0:T(8,128)} %rhs.1, f32[1,2,32,1024]{3,2,1,0:T(8,128)} %err.1, f32[4,1,2,32,1024]{4,3,2,1,0:T(8,128)} %cof.1, s32[1,32]{1,0:T(1,128)} %oblk_in.1, s32[1,32,128]{2,1,0:T(8,128)} %opos_in.1, f32[1,32,128]{2,1,0:T(8,128)} %owgt_in.1), custom_call_target="tpu_custom_call" | custom-call | tf_op jit(solution)/shard_map/pallas_call | solution.py:739
  38.5 0.7 %copy.10 = f32[1,2,32,1024]{3,2,1,0:T(8,128)} copy(f32[1,2,32,1024]{3,2,1,0:T(8,128)S(1)} %get-tuple-element.2) | data formatting | bytes 524288
  39.2 0.7 %copy.11 = f32[1,2,32,1024]{3,2,1,0:T(8,128)} copy(f32[1,2,32,1024]{3,2,1,0:T(8,128)S(1)} %get-tuple-element.3) | data formatting | bytes 524288
